TPU v7x, 512 devices: a whole 4x8x8 slice. The times are simulated.
512 devices in a mesh: lat: 128 (over y, x_lo, z), lev: 4 (over x_hi, core).
Axes of the slice: x: 4 (x_hi: 2, x_lo: 2; x = x_hi * 2 + x_lo), y: 8, z: 8, core: 2. Of those that a mesh axis runs over, the one named last changes fastest.
Arguments:
- assign: int32 [640], replicated, may hold values from 0 to 639, each once
- u_spec: bfloat16 [640, 32, 2, 640], P('lat', 'lev'), may hold values from -0.25 to 0.25
- v_spec: bfloat16 [640, 32, 2, 640], P('lat', 'lev'), may hold values from -0.25 to 0.25
- basis: bfloat16 [640, 640, 640], P('lat', 'lev'), may hold values from -0.25 to 0.25
Outputs:
- vort_spec: float32 [640, 32, 2, 640], P('lat', 'lev')
Inputs may be any that keep to these rules, and one draw needn't show every extreme that they name: Row k of u_spec, v_spec, basis and vort_spec belongs to zonal wavenumber assign[k]; each of the 640 wavenumbers appears once.
All inputs are finite; a program needn't handle non-finite values.
Results may differ from a plain program's by a relative error of at most 0.0061.
Values may be sent and summed in bfloat16 or wider, within the bound.
A program may use at most 64 MiB of HBM per device.

v0:
```python
import math

import jax
import jax.numpy as jnp
from jax import lax
from jax.sharding import PartitionSpec as P

M = 640
LAT = 1280
LON = 2560


def padded_2(block, sides, width):
    for axis, dim in sides:
        count = lax.axis_size(axis)
        forward = [(i, i + 1) for i in range(count - 1)]
        backward = [(target, source) for source, target in forward]
        low = lax.ppermute(
            lax.slice_in_dim(block, block.shape[dim] - width, None, axis=dim), axis, forward
        )
        high = lax.ppermute(lax.slice_in_dim(block, 0, width, axis=dim), axis, backward)
        block = jnp.concatenate([low, block, high], axis=dim)
    return block


def degree_factors(wavenums):
    degree = jnp.arange(M, dtype=jnp.int32)
    live_mask = (degree[None, :] >= wavenums[:, None]).astype(jnp.int32)
    parity = 1 - 2 * ((degree[None, :] + wavenums[:, None]) % 2)
    return (live_mask, live_mask * parity)


def zonal_tables(wavenums):
    columns = jnp.arange(LON, dtype=jnp.int32)
    phases = wavenums[:, None] * columns[None, :] % LON
    angles = phases.astype(jnp.float32) * (2.0 * math.pi / LON)
    return jnp.stack([jnp.cos(angles), jnp.sin(angles)], axis=0).astype(jnp.bfloat16)


def body(assign, u_spec, v_spec, basis):
    slot_count = u_spec.shape[0]
    lev_dev = u_spec.shape[1]
    lat_count = lax.axis_size("lat")
    half_rows = LAT // 2
    row_count = LAT // lat_count
    lat_index = lax.axis_index("lat")
    my_waves = lax.dynamic_slice_in_dim(assign, lat_index * slot_count, slot_count)
    live_mask, signed = degree_factors(my_waves)
    live_half = live_mask.astype(jnp.bfloat16)[:, None, :]
    signed_half = signed.astype(jnp.bfloat16)[:, None, :]
    live_full = live_mask.astype(jnp.float32)[:, None, :]
    signed_full = signed.astype(jnp.float32)[:, None, :]
    basis_all = lax.all_gather(basis, "lev", axis=1, tiled=True)
    spectra = jnp.stack([u_spec, v_spec], axis=2).reshape(slot_count, lev_dev * 4, M)
    northern = jnp.einsum(
        "kcn,kjn->kcj", spectra * live_half, basis_all, preferred_element_type=jnp.float32
    )
    southern = jnp.einsum(
        "kcn,kjn->kcj", spectra * signed_half, basis_all, preferred_element_type=jnp.float32
    )[:, :, ::-1]
    fourier = jnp.concatenate([northern, southern], axis=2).astype(jnp.bfloat16)
    incoming = lax.all_to_all(fourier, "lat", split_axis=2, concat_axis=0, tiled=True)
    incoming = incoming.reshape(M, lev_dev, 2, 2, row_count)
    zonal_table = zonal_tables(assign)
    grid_fields = jnp.einsum(
        "klfcj,ckq->fljq", incoming, zonal_table, preferred_element_type=jnp.float32
    )
    scaled = grid_fields[0]
    padded = padded_2(scaled, (("lat", 1),), 1)
    upper_row = jnp.where(lat_index == 0, -jnp.roll(scaled[:, 0], LON // 2, axis=-1), padded[:, 0])
    lower_row = jnp.where(
        lat_index == lat_count - 1, -jnp.roll(scaled[:, -1], LON // 2, axis=-1), padded[:, -1]
    )
    row_above = jnp.concatenate([upper_row[:, None], scaled[:, :-1]], axis=1)
    row_below = jnp.concatenate([scaled[:, 1:], lower_row[:, None]], axis=1)
    merid_v = grid_fields[1]
    vorticity = 0.5 * (jnp.roll(merid_v, -1, axis=-1) - jnp.roll(merid_v, 1, axis=-1)) - 0.5 * (
        row_above - row_below
    )
    flux = (vorticity * scaled).astype(jnp.bfloat16)
    zonal_back = jnp.einsum(
        "ljq,ckq->klcj", flux, zonal_table, preferred_element_type=jnp.float32
    ) * (1.0 / math.sqrt(LON))
    zonal_back = zonal_back.astype(jnp.bfloat16).reshape(M, lev_dev * 2, row_count)
    returned = lax.all_to_all(zonal_back, "lat", split_axis=0, concat_axis=2, tiled=True)
    northern = jnp.einsum(
        "kjn,kcj->kcn", basis_all, returned[:, :, :half_rows], preferred_element_type=jnp.float32
    )
    southern = jnp.einsum(
        "kjn,kcj->kcn",
        basis_all,
        returned[:, :, half_rows:][:, :, ::-1],
        preferred_element_type=jnp.float32,
    )
    combined = live_full * northern + signed_full * southern
    result = combined.reshape(slot_count, lev_dev, 2, M)
    return result


def solution(mesh):
    return jax.shard_map(
        body,
        mesh=mesh,
        in_specs=(
            P(),
            P("lat", "lev", None, None),
            P("lat", "lev", None, None),
            P("lat", "lev", None),
        ),
        out_specs=P("lat", "lev", None, None),
        check_vma=False,
    )
```

profile of v0, /device:TPU:6, one launch (start us, length us, event | category | flops | bytes accessed | tf_op | source)
XLA Modules:
  0.0 200.2 jit_solution(4600741148534901010)
XLA Ops:
  7.3 1.2 pad_maximum_fusion.4
  8.8 0.8 dynamic_slice.3
  9.7 46.1 %all-gather.2.cloned.1.call-done = bf16[5,640,640]{2,1,0:T(8,128)(2,1)} async-done(((bf16[5,160,640]{2,1,0:T(8,128)(2,1)}), bf16[5,640,640]{2,1,0:T(8,128)(2,1)}) %all-gather.2.cloned.1.call-update) | async-done | bytes 4096016 | tf_op jit(solution)/shard_map/all_gather | solution.py:53
  55.8 3.5 %fusion.32 = bf16[5,32,640]{2,1,0:T(8,128)(2,1)S(1)} fusion(bf16[5,640,640]{2,1,0:T(8,128)(2,1)} %all-gather.2.cloned.1.call-done, bf16[5,32,640]{2,1,0:T(8,128)(2,1)S(1)} %reshape.252, bf16[5,640]{1,0:T(8,128)(2,1)S(1)} %get-tuple-element.26), kind=kOutput, calls=%fused_computation.35 | convolution fusion | flops 131174400 | bytes 4512000 | tf_op jit(solution)/shard_map/kcn,kjn->kcj/dot_general | solution.py:58
  59.9 3.5 %convolution_convert_fusion = bf16[5,32,640]{2,1,0:T(8,128)(2,1)S(1)} fusion(bf16[5,640,640]{2,1,0:T(8,128)(2,1)} %all-gather.2.cloned.1.call-done, bf16[5,32,640]{2,1,0:T(8,128)(2,1)S(1)} %reshape.252, bf16[5,640]{1,0:T(8,128)(2,1)S(1)} %get-tuple-element.24), kind=kOutput, calls=%fused_computation.28 | convolution fusion | flops 131276800 | bytes 4512000 | tf_op jit(solution)/shard_map/kcn,kjn->kcj/dot_general | solution.py:55
  63.4 1.8 copy.22
  65.2 2.4 %reshape.260 = bf16[128,2,800]{2,1,0:T(2,128)(2,1)} reshape(bf16[1280,5,32]{2,1,0:T(8,128)(2,1)S(1)} %bitcast.75) | data formatting | bytes 819200
  67.6 15.1 %all-to-all-start = ((bf16[128,2,800]{2,1,0:T(2,128)(2,1)}), bf16[128,2,800]{2,1,0:T(2,128)(2,1)S(1)}, u32[]{:S(2)}, u32[]{:S(2)}) async-start(bf16[128,2,800]{2,1,0:T(2,128)(2,1)} %reshape.260), calls=%async_computation | async-start | bytes 917504 | tf_op jit(solution)/shard_map/all_to_all | solution.py:62
  82.7 29.2 %cosine_convert_fusion = (bf16[1,640,2560]{2,1,0:T(8,128)(2,1)}, bf16[1,640,2560]{2,1,0:T(8,128)(2,1)}) fusion(s32[640]{0:T(1024)S(1)} %copy-done.3), kind=kLoop, calls=%fused_computation.9 | loop fusion | flops 18022400 | bytes 6556160 | tf_op jit(solution)/shard_map/convert.2
  111.9 1.8 reshape.261
  113.7 6.9 %copy.24 = bf16[128,5,32,10]{3,2,1,0:T(8,128)(2,1)} copy(bf16[128,5,32,10]{2,1,3,0:T(8,128)(2,1)S(1)} %bitcast.78) | data formatting | bytes 819200 | tf_op jit(solution)/shard_map/all_to_all | solution.py:62
  120.6 8.8 %fusion.10 = f32[2,8,10,2560]{3,2,0,1:T(8,128)S(1)} fusion(bf16[640,8,2,2,10]{4,3,2,1,0:T(2,128)(2,1)} %bitcast.79, bf16[1,640,2560]{2,1,0:T(8,128)(2,1)} %get-tuple-element.22, bf16[1,640,2560]{2,1,0:T(8,128)(2,1)} %get-tuple-element.21), kind=kOutput, calls=%fused_computation.15 | convolution fusion | flops 1061683200 | bytes 8601600 | tf_op jit(solution)/shard_map/klfcj,ckq->fljq/dot_general | solution.py:65
  129.7 4.6 %collective-permute-start.1 = (f32[8,1,2560]{2,1,0:T(1,128)S(1)}, f32[8,1,2560]{2,1,0:T(1,128)S(1)}, u32[]{:S(2)}, u32[]{:S(2)}) collective-permute-start(f32[8,1,2560]{2,1,0:T(1,128)S(1)} %get-tuple-element.9), channel_id=1, source_target_pairs={{4,0},{8,4},{12,8},{16,12},{20,16},{24,20},{28,24},{32,28},{36,32}... | collective-permute-start | bytes 245768 | tf_op jit(solution)/shard_map/ppermute | solution.py:21
  135.1 2.2 %collective-permute-start = (f32[8,1,2560]{2,0,1:T(8,128)S(1)}, f32[8,1,2560]{2,0,1:T(8,128)S(1)}, u32[]{:S(2)}, u32[]{:S(2)}) collective-permute-start(f32[8,1,2560]{2,0,1:T(8,128)S(1)} %copy.53), channel_id=1, source_target_pairs={{0,4},{4,8},{8,12},{12,16},{16,20},{20,24},{24,28},{28,32},{32,36}... | collective-permute-start | bytes 245768 | tf_op jit(solution)/shard_map/ppermute | solution.py:18
  137.4 6.5 %collective-permute-done = f32[8,1,2560]{2,0,1:T(8,128)S(1)} collective-permute-done((f32[8,1,2560]{2,0,1:T(8,128)S(1)}, f32[8,1,2560]{2,0,1:T(8,128)S(1)}, u32[]{:S(2)}, u32[]{:S(2)}) %collective-permute-start) | collective-permute-done | bytes 81952 | tf_op jit(solution)/shard_map/ppermute | solution.py:18
  144.1 2.5 %fusion.26 = bf16[640,8,2,10]{0,3,1,2:T(8,128)(2,1)S(1)} fusion(bf16[1,640,2560]{2,1,0:T(8,128)(2,1)S(1)} %copy-done.2, bf16[1,640,2560]{2,1,0:T(8,128)(2,1)S(1)} %copy-done.1, f32[8,10,1]{2,1,0:T(8,128)S(1)} %get-tuple-element.12, f32[8,10,2559]{2,1,0:T(8,128)S(1)} %get-tuple-element.14, f32[8,10,2559]{2,1,0:T(8,128)S(1)} %get-tuple-element.13, ...), kind=kOutput, calls=%fused_computation.27 | convolution fusion | flops 539852800 | bytes 13606912 | tf_op jit(solution)/shard_map/ljq,ckq->klcj/dot_general | solution.py:81
  146.9 2.1 %copy.31 = bf16[640,16,10]{1,2,0:T(8,128)(2,1)S(1)} copy(bf16[640,16,10]{0,1,2:T(8,128)(2,1)S(1)} %reshape.254) | data formatting | bytes 409600 | tf_op jit(solution)/shard_map/reshape | solution.py:84
  149.0 1.7 reshape.262
  150.7 25.0 %all_to_all.33 = bf16[128,2,400]{2,1,0:T(2,128)(2,1)S(1)} all-to-all(bf16[128,2,400]{2,1,0:T(2,128)(2,1)S(1)} %reshape.262), channel_id=1, replica_groups=mesh['lat'=128,'lev'=4] {'lat'}, dimensions={0} | all-to-all | bytes 409600 | tf_op jit(solution)/shard_map/all_to_all | solution.py:85
  175.8 1.4 reshape.263
  177.1 6.3 %copy.33 = bf16[5,16,128,10]{3,2,1,0:T(8,128)(2,1)} copy(bf16[5,16,128,10]{1,3,0,2:T(8,128)(2,1)S(1)} %bitcast.77) | data formatting | bytes 409600 | tf_op jit(solution)/shard_map/all_to_all | solution.py:85
  183.4 4.5 %all_to_all.30 = bf16[5,16,1280]{2,1,0:T(8,128)(2,1)S(1)} reshape(bf16[5,16,128,10]{3,2,1,0:T(8,128)(2,1)} %copy.33) | data formatting | bytes 409600 | tf_op jit(solution)/shard_map/all_to_all | solution.py:85
  188.5 3.0 %convolution_multiply_fusion = f32[5,16,640]{2,1,0:T(8,128)S(1)} fusion(bf16[5,16,640]{2,1,0:T(8,128)(2,1)S(1)} %rev.7, bf16[5,640,640]{2,1,0:T(8,128)(2,1)} %all-gather.2.cloned.1.call-done, f32[5,640]{1,0:T(8,128)S(1)} %get-tuple-element.25), kind=kOutput, calls=%fused_computation.29 | convolution fusion | flops 65587200 | bytes 4416000 | tf_op jit(solution)/shard_map/kjn,kcj->kcn/dot_general | solution.py:89
  192.5 0.8 reshape.255
  (36 shorter events, 4.9 us)
Async XLA Ops:
  6.5 49.3 %all-gather.2.cloned.1.call-start = ((), (), s32[]{:S(2)}) async-start(), calls=%async_computation.2 | async-start | bytes 5120000 | tf_op jit(solution)/shard_map/all_gather | solution.py:53
  63.4 19.3 %copy-start.3 = (s32[640]{0:T(1024)S(1)}, s32[640]{0:T(1024)}, u32[]{:S(2)}) copy-start(s32[640]{0:T(1024)} %param.4) | copy-start | bytes 7684
  67.6 44.3 %all-to-all-start = ((bf16[128,2,800]{2,1,0:T(2,128)(2,1)}), bf16[128,2,800]{2,1,0:T(2,128)(2,1)S(1)}, u32[]{:S(2)}, u32[]{:S(2)}) async-start(bf16[128,2,800]{2,1,0:T(2,128)(2,1)} %reshape.260), calls=%async_computation | async-start | bytes 917504 | tf_op jit(solution)/shard_map/all_to_all | solution.py:62
  129.7 14.2 %collective-permute-start.1 = (f32[8,1,2560]{2,1,0:T(1,128)S(1)}, f32[8,1,2560]{2,1,0:T(1,128)S(1)}, u32[]{:S(2)}, u32[]{:S(2)}) collective-permute-start(f32[8,1,2560]{2,1,0:T(1,128)S(1)} %get-tuple-element.9), channel_id=1, source_target_pairs={{4,0},{8,4},{12,8},{16,12},{20,16},{24,20},{28,24},{32,28},{36,32}... | collective-permute-start | bytes 245768 | tf_op jit(solution)/shard_map/ppermute | solution.py:21
  134.6 9.4 %copy-start.1 = (bf16[1,640,2560]{2,1,0:T(8,128)(2,1)S(1)}, bf16[1,640,2560]{2,1,0:T(8,128)(2,1)}, u32[]{:S(2)}) copy-start(bf16[1,640,2560]{2,1,0:T(8,128)(2,1)} %get-tuple-element.21) | copy-start | bytes 9830404
  134.6 9.4 %copy-start.2 = (bf16[1,640,2560]{2,1,0:T(8,128)(2,1)S(1)}, bf16[1,640,2560]{2,1,0:T(8,128)(2,1)}, u32[]{:S(2)}) copy-start(bf16[1,640,2560]{2,1,0:T(8,128)(2,1)} %get-tuple-element.22) | copy-start | bytes 9830404
  135.1 8.7 %collective-permute-start = (f32[8,1,2560]{2,0,1:T(8,128)S(1)}, f32[8,1,2560]{2,0,1:T(8,128)S(1)}, u32[]{:S(2)}, u32[]{:S(2)}) collective-permute-start(f32[8,1,2560]{2,0,1:T(8,128)S(1)} %copy.53), channel_id=1, source_target_pairs={{0,4},{4,8},{8,12},{12,16},{16,20},{20,24},{24,28},{28,32},{32,36}... | collective-permute-start | bytes 245768 | tf_op jit(solution)/shard_map/ppermute | solution.py:18
  188.4 3.4 %copy-start = (bf16[5,640,640]{2,1,0:T(8,128)(2,1)S(1)}, bf16[5,640,640]{2,1,0:T(8,128)(2,1)}, u32[]{:S(2)}) copy-start(bf16[5,640,640]{2,1,0:T(8,128)(2,1)} %all-gather.2.cloned.1.call-done) | copy-start | bytes 12288004
Sparse Core Ops, SparseCore 0:
  9.4 46.3 all-gather.1
where the time goes:
time: 202 us; the launch traced here: 200 us
  waiting for transfers between devices  53.3 us (26%)
  local copies, waits for them, and re-layouts  33.5 us (17%)
  other arithmetic  30.8 us (15%)
  blocking collectives  25 us (12%)
  starting transfers between devices  21.9 us (11%)
  matrix products  21.9 us (11%)
  between operations  13.7 us (7%)
    all_gather x1, waiting for transfers between devices, body(): basis_all = lax.all_gather(basis, 'lev', axis=1, tiled=True)  46.1 us
    another operation x1, other arithmetic  29.2 us
    all_to_all x1, blocking collectives, body(): lax.all_to_all(zonal_back, 'lat', split_axis=0, concat_axis=2, tiled=True)  25 us
    all_to_all x1, starting transfers between devices, body(): lax.all_to_all(fourier, 'lat', split_axis=2, concat_axis=0, tiled=True)  15.1 us
    all_to_all x2, local copies, waits for them, and re-layouts, body(): lax.all_to_all(zonal_back, 'lat', split_axis=0, concat_axis=2, tiled=True)  10.8 us
    dot_general x1, matrix products, body(): jnp.einsum('klfcj,ckq->fljq', incoming, zonal_table, preferred_element_ty...  8.82 us
    unnamed x13, local copies, waits for them, and re-layouts  7.72 us
    all_to_all x1, local copies, waits for them, and re-layouts, body(): lax.all_to_all(fourier, 'lat', split_axis=2, concat_axis=0, tiled=True)  6.88 us
  transfers between devices with their start and end apart: 4, of which 2 were waited for; matrix products, arithmetic and copies ran while one was open for 16% of the time, Pallas kernels for 0%

commit v1 on v0

v1 whole, which is shorter than its diff:
```python
import functools
import math

import jax
import jax.numpy as jnp
from jax import lax
from jax.experimental import pallas as pl
from jax.experimental.pallas import tpu as pltpu
from jax.sharding import PartitionSpec as P

LON = 2560
SLOTS = 5
BLOCKS = 5
LANES = 128
PARTNER_CORE = [(0, 1), (1, 0), (2, 3), (3, 2)]
PARTNER_X = [(0, 2), (2, 0), (1, 3), (3, 1)]


def cos_sin(turns):
    x = turns - jnp.floor(turns + 0.5)
    u = x * x
    cos = jnp.full_like(u, (2 * math.pi) ** 18 / math.factorial(18) * -1.0)
    sin = jnp.full_like(u, (2 * math.pi) ** 19 / math.factorial(19) * -1.0)
    for i in range(8, -1, -1):
        sign = 1.0 if i % 2 == 0 else -1.0
        cos = cos * u + sign * (2 * math.pi) ** (2 * i) / math.factorial(2 * i)
        sin = sin * u + sign * (2 * math.pi) ** (2 * i + 1) / math.factorial(2 * i + 1)
    return cos, sin * x


def kernel(
    n_lat, rows_x, levels, degrees,
    waves_ref, factors_ref, lhs_ref, basis_ref, lane_waves_ref, row_waves_ref,
    out_ref,
    send, recv, coeffs, flux, back, ret, sum_send, sum_recv, table_q, table_k,
    send_sem, recv_sem, local_sem, back_send_sem, back_recv_sem, back_local_sem, sum_send_sem, sum_recv_sem,
):
    me = lax.axis_index("lat")
    lev = lax.axis_index("lev")
    x_hi = lev // 2
    groups = n_lat // 8
    units = BLOCKS * levels
    pair = 2 * levels
    spread = 2 * lev
    wide = basis_ref.shape[1]
    total = SLOTS * n_lat * 2

    my_group = me // 8
    my_z = lax.rem(lax.rem(me, 8) + 32 - lax.rem(my_group * 3 + spread, 8), 8)
    my_entry = (5 * my_z + 7) // 8
    active = (8 * my_entry) // 5 == my_z
    my_unit = my_group * 5 + my_entry
    my_block = my_unit // levels
    my_level = lax.rem(my_unit, levels)

    def owner_of(unit):
        group = unit // 5
        entry = lax.rem(unit, 5)
        return group * 8 + lax.rem((8 * entry) // 5 + lax.rem(group * 3 + spread, 8), 8)

    barrier = pltpu.get_barrier_semaphore()

    @pl.loop(1, n_lat)
    def _(i):
        pl.semaphore_signal(barrier, inc=1, device_id={"lat": lax.rem(me + i, n_lat)}, device_id_type=pl.DeviceIdType.MESH)

    partner = lax.rem(lev + 2, 4)
    pl.semaphore_signal(barrier, inc=1, device_id={"lev": partner}, device_id_type=pl.DeviceIdType.MESH)

    send_rows = send.reshape(2, BLOCKS, SLOTS, pair, LANES)
    lane = lax.broadcasted_iota(jnp.int32, (2 * pair, wide), 1)
    row = lax.broadcasted_iota(jnp.int32, (2 * pair, wide), 0)
    half_sign = jnp.where(row < pair, -0.5, 0.5)
    lane_tile = lax.broadcasted_iota(jnp.int32, (pair, LANES), 1)

    @pl.loop(0, SLOTS)
    def _(k):
        fields = lax.dot_general(
            lhs_ref[k], basis_ref[k], (((1,), (1,)), ((), ())), preferred_element_type=jnp.float32
        )
        wind = fields[: 2 * pair]
        other = fields[2 * pair :]
        before = pltpu.roll(wind, 1, 1)
        after = pltpu.roll(wind, wide - 1, 1)
        swapped = jnp.concatenate([wind[pair:], wind[:pair]], axis=0)
        before = jnp.where((lane == 0) & (x_hi == 0), -factors_ref[1, k] * wind, before)
        after = jnp.where((lane == rows_x - 1) & (x_hi == 1), swapped, after)
        curl = factors_ref[0, k] * other + half_sign * (before - after)
        for f, value in enumerate((wind, curl)):
            north, south = value[:pair], value[pair:]
            tail = 2 * LANES
            mixed = jnp.where(
                lane_tile < LANES // 2,
                north[:, tail : tail + LANES],
                pltpu.roll(south[:, tail : tail + LANES], LANES // 2, 1),
            )
            tiles = (north[:, :LANES], north[:, LANES:tail], south[:, :LANES], south[:, LANES:tail], mixed)
            for b, tile in enumerate(tiles):
                send_rows[f, b, k] = tile.astype(jnp.bfloat16)

    chunk = min(64, total)

    @pl.loop(0, total // chunk)
    def _(i):
        rows = pl.ds(pl.multiple_of(i * chunk, chunk), chunk)
        wave = row_waves_ref[rows, :]
        column = lax.broadcasted_iota(jnp.int32, (chunk, LANES), 1).astype(jnp.float32)
        part = lax.broadcasted_iota(jnp.int32, (chunk, LANES), 0)
        shift = (part - 2 * (part // 2)).astype(jnp.float32) * 0.25
        cos, sin = cos_sin(wave * column * (1.0 / LON) - shift)
        turn_cos, turn_sin = cos_sin(wave * (LANES / LON))
        for step in range(LON // LANES):
            table_k[rows, step * LANES : (step + 1) * LANES] = cos.astype(jnp.bfloat16)
            cos, sin = cos * turn_cos - sin * turn_sin, sin * turn_cos + cos * turn_sin

    pl.semaphore_wait(barrier, n_lat)

    first = (me * 5) // 8

    def unit_copy(unit):
        block = unit // levels
        level = lax.rem(unit, levels)
        return send.at[:, block, :, level], owner_of(unit)

    @pl.loop(0, units)
    def _(i):
        unit = lax.rem(first + i, units)
        source, owner = unit_copy(unit)

        @pl.when(owner != me)
        def _():
            pltpu.make_async_remote_copy(
                src_ref=source, dst_ref=recv.at[:, me], send_sem=send_sem, recv_sem=recv_sem,
                device_id={"lat": owner}, device_id_type=pl.DeviceIdType.MESH,
            ).start()

        @pl.when(owner == me)
        def _():
            pltpu.make_async_copy(source, recv.at[:, me], local_sem).start()

    width = total // 2
    for part in range(2):
        lanes = pl.ds(part * width, width)
        height = 16
        wave = jnp.broadcast_to(lane_waves_ref[0:1, lanes], (height, width))
        position = lax.broadcasted_iota(jnp.int32, (height, width), 0).astype(jnp.float32)
        side = lax.broadcasted_iota(jnp.int32, (height, width), 1)
        shift = (side - 2 * (side // 2)).astype(jnp.float32) * 0.25
        start = cos_sin(wave * position * (1.0 / LON) - shift)
        turn_cos, turn_sin = cos_sin(lane_waves_ref[0:8, lanes] * (height / LON))
        turn_cos = jnp.concatenate([turn_cos] * (height // 8), axis=0)
        turn_sin = jnp.concatenate([turn_sin] * (height // 8), axis=0)

        def advance(i, carry):
            cos, sin = carry
            table_q[pl.ds(pl.multiple_of(i * height, height), height), lanes] = cos.astype(jnp.bfloat16)
            return cos * turn_cos - sin * turn_sin, sin * turn_cos + cos * turn_sin

        lax.fori_loop(0, LON // height, advance, start)

    @pl.when(active)
    def _():
        remote = recv.at[:, pl.ds(0, n_lat - 1)]
        pltpu.make_async_copy(remote, remote, recv_sem).wait()
        pltpu.make_async_copy(recv.at[:, 0], recv.at[:, 0], local_sem).wait()
        recv_rows = recv.reshape(2, total, LANES)
        coeffs[:, :LANES] = recv_rows[0]
        coeffs[:, LANES:] = recv_rows[1]
        step = 256

        @pl.loop(0, LON // step)
        def _(i):
            rows = pl.ds(pl.multiple_of(i * step, step), step)
            grid = jnp.dot(table_q[rows, :], coeffs[...], preferred_element_type=jnp.float32)
            flux[rows, :] = (grid[:, :LANES] * grid[:, LANES:]).astype(jnp.bfloat16)

        back_rows = back.reshape(total, LANES)
        high = min(256, total)

        @pl.loop(0, total // high)
        def _(i):
            rows = pl.ds(pl.multiple_of(i * high, high), high)
            zonal = jnp.dot(table_k[rows, :], flux[...], preferred_element_type=jnp.float32)
            back_rows[rows, :] = (zonal * (1.0 / math.sqrt(LON))).astype(jnp.bfloat16)

        @pl.loop(1, n_lat)
        def _(i):
            owner = lax.rem(me + i, n_lat)
            pltpu.make_async_remote_copy(
                src_ref=back.at[owner], dst_ref=ret.at[my_block, :, my_level],
                send_sem=back_send_sem, recv_sem=back_recv_sem,
                device_id={"lat": owner}, device_id_type=pl.DeviceIdType.MESH,
            ).start()

        own = pltpu.make_async_copy(back.at[me], ret.at[my_block, :, my_level], back_local_sem)
        own.start()
        own.wait()
        sent = recv.at[:, pl.ds(0, units - 1)]
        pltpu.make_async_copy(sent, sent, send_sem).wait()
        got = recv.at[0, pl.ds(0, units - 1)]
        pltpu.make_async_copy(got, got, back_recv_sem).wait()

    @pl.when(jnp.logical_not(active))
    def _():
        sent = recv.at[:, pl.ds(0, units)]
        pltpu.make_async_copy(sent, sent, send_sem).wait()
        got = recv.at[0, pl.ds(0, units)]
        pltpu.make_async_copy(got, got, back_recv_sem).wait()

    ret_rows = ret.reshape(BLOCKS, SLOTS, pair, LANES)
    degree = lax.broadcasted_iota(jnp.int32, (pair, degrees), 1)
    degree_sign = jnp.where(lax.rem(degree, 2) == 0, 1.0, -1.0)

    def sum_copy(k):
        return pltpu.make_async_remote_copy(
            src_ref=sum_send.at[k], dst_ref=sum_recv.at[k],
            send_sem=sum_send_sem.at[k], recv_sem=sum_recv_sem.at[k],
            device_id={"lev": partner}, device_id_type=pl.DeviceIdType.MESH,
        )

    @pl.loop(0, SLOTS)
    def _(k):
        mixed = ret_rows[4, k].astype(jnp.float32)
        zero = jnp.zeros_like(mixed)
        tail_north = jnp.where(lane_tile < LANES // 2, mixed, zero).astype(jnp.bfloat16)
        tail_south = jnp.where(lane_tile < LANES // 2, pltpu.roll(mixed, LANES // 2, 1), zero).astype(jnp.bfloat16)
        north = jnp.concatenate([ret_rows[0, k], ret_rows[1, k], tail_north], axis=1)
        south = jnp.concatenate([ret_rows[2, k], ret_rows[3, k], tail_south], axis=1)
        both = jnp.dot(
            jnp.concatenate([north, south], axis=0), basis_ref[k], preferred_element_type=jnp.float32
        )
        combined = both[:pair] + (factors_ref[1, k] * degree_sign) * both[pair:]
        combined = jnp.where(degree >= waves_ref[k], combined, 0.0)
        low, high = combined[:levels], combined[levels:]
        out_ref[k] = jnp.where(x_hi == 0, low, high)
        sum_send[k] = jnp.where(x_hi == 0, high, low).astype(jnp.bfloat16)
        sum_copy(k).start()

    @pl.when(active)
    def _():
        sent = recv.at[0, pl.ds(0, n_lat - 1)]
        pltpu.make_async_copy(sent, sent, back_send_sem).wait()

    @pl.loop(0, SLOTS)
    def _(k):
        copy = sum_copy(k)
        copy.wait()
        out_ref[k] += sum_recv[k].astype(jnp.float32)


def body(n_lat, assign, u_spec, v_spec, basis):
    slots, lev_dev, _, degrees = u_spec.shape
    lev = lax.axis_index("lev")
    x_hi = lev // 2
    core = lev % 2
    levels = 2 * lev_dev
    waves = lax.dynamic_slice_in_dim(assign, lax.axis_index("lat") * slots, slots)

    edge = jnp.where(lev == 2, basis[:, 0], basis[:, -1])
    halo = lax.ppermute(edge, "lev", [(2, 0), (1, 3)]) + lax.ppermute(edge, "lev", [(2, 1), (1, 2)])
    other_basis = lax.ppermute(basis, "lev", PARTNER_CORE)
    other_u = lax.ppermute(u_spec, "lev", PARTNER_X)
    other_v = lax.ppermute(v_spec, "lev", PARTNER_X)

    rows_x = 2 * basis.shape[1]
    low = jnp.where(core == 0, basis, other_basis)
    high = jnp.where(core == 0, other_basis, basis)
    halo_rows = jnp.broadcast_to(halo[:, None], (slots, 64, degrees))
    basis_wide = jnp.concatenate([low, high, halo_rows], axis=1)

    def joined(mine, other):
        first = jnp.where(x_hi == 0, mine, other)
        second = jnp.where(x_hi == 0, other, mine)
        return jnp.concatenate([first, second], axis=1)

    u_all = joined(u_spec, other_u)
    v_all = joined(v_spec, other_v)
    v_turned = jnp.stack([v_all[:, :, 1], -v_all[:, :, 0]], axis=2)
    degree = jnp.arange(degrees, dtype=jnp.int32)
    live = (degree[None, :] >= waves[:, None]).astype(jnp.bfloat16)
    sign = (1 - 2 * ((degree[None, :] + waves[:, None]) % 2)).astype(jnp.bfloat16) * live
    masks = jnp.stack([live, sign], axis=1)[:, None, :, None, :]
    spectra = jnp.stack([u_all, v_turned], axis=1).reshape(slots, 2, 1, 2 * levels, degrees)
    lhs = (spectra * masks).reshape(slots, 8 * levels, degrees)

    angle = waves.astype(jnp.float32) * (2.0 * math.pi / LON)
    factors = jnp.stack([jnp.sin(angle), (1 - 2 * (waves % 2)).astype(jnp.float32)])
    order = jnp.repeat(assign.astype(jnp.float32), 2)
    total = order.shape[0]
    lane_waves = jnp.broadcast_to(order[None, :], (8, total))
    row_waves = jnp.broadcast_to(order[:, None], (total, LANES))

    vmem = pl.BlockSpec(memory_space=pltpu.VMEM)
    smem = pl.BlockSpec(memory_space=pltpu.SMEM)
    result = pl.pallas_call(
        functools.partial(kernel, n_lat, rows_x, levels, degrees),
        out_shape=jax.ShapeDtypeStruct((slots, levels, degrees), jnp.float32),
        in_specs=[smem, smem, vmem, vmem, vmem, vmem],
        out_specs=vmem,
        scratch_shapes=[
            pltpu.VMEM((2, BLOCKS, SLOTS, levels, 2, LANES), jnp.bfloat16),
            pltpu.VMEM((2, n_lat, SLOTS, 2, LANES), jnp.bfloat16),
            pltpu.VMEM((total, 2 * LANES), jnp.bfloat16),
            pltpu.VMEM((LON, LANES), jnp.bfloat16),
            pltpu.VMEM((n_lat, SLOTS, 2, LANES), jnp.bfloat16),
            pltpu.VMEM((BLOCKS, SLOTS, levels, 2, LANES), jnp.bfloat16),
            pltpu.VMEM((SLOTS, levels, degrees), jnp.bfloat16),
            pltpu.VMEM((SLOTS, levels, degrees), jnp.bfloat16),
            pltpu.VMEM((LON, total), jnp.bfloat16),
            pltpu.VMEM((total, LON), jnp.bfloat16),
            pltpu.SemaphoreType.DMA,
            pltpu.SemaphoreType.DMA,
            pltpu.SemaphoreType.DMA,
            pltpu.SemaphoreType.DMA,
            pltpu.SemaphoreType.DMA,
            pltpu.SemaphoreType.DMA,
            pltpu.SemaphoreType.DMA((SLOTS,)),
            pltpu.SemaphoreType.DMA((SLOTS,)),
        ],
        compiler_params=pltpu.CompilerParams(
            collective_id=0, has_side_effects=True, vmem_limit_bytes=48 * 1024 * 1024
        ),
    )(waves, factors, lhs, basis_wide, lane_waves, row_waves)
    return result.reshape(slots, lev_dev, 2, degrees)


def solution(mesh):
    return jax.shard_map(
        functools.partial(body, mesh.shape["lat"]),
        mesh=mesh,
        in_specs=(
            P(),
            P("lat", "lev", None, None),
            P("lat", "lev", None, None),
            P("lat", "lev", None),
        ),
        out_specs=P("lat", "lev", None, None),
        check_vma=False,
    )
```

time: 202 us -> 84.1 us (0.42)
  the two profiles are of different devices: /device:TPU:6 before, /device:TPU:2 now
where the time goes in v1:
time: 84.1 us; the launch traced here: 83.7 us
  Pallas kernels  57.3 us (68%)
  starting transfers between devices  15 us (18%)
  other arithmetic  4.57 us (5%)
  waiting for transfers between devices  4.13 us (5%)
  local copies, waits for them, and re-layouts  2.42 us (3%)
    pallas_call x1, Pallas kernels, body(): pl.pallas_call(functools.partial(kernel, n_lat, rows_x, levels, degrees),...  57.3 us
    ppermute x1, starting transfers between devices, body(): other_v = lax.ppermute(v_spec, 'lev', PARTNER_X)  9.25 us
    ppermute x1, waiting for transfers between devices, body(): other_u = lax.ppermute(u_spec, 'lev', PARTNER_X)  4.12 us
    ppermute x1, starting transfers between devices, body(): other_u = lax.ppermute(u_spec, 'lev', PARTNER_X)  1.92 us
    ppermute x1, starting transfers between devices, body(): other_basis = lax.ppermute(basis, 'lev', PARTNER_CORE)  1.91 us
  transfers between devices with their start and end apart: 5, of which 1 were waited for; matrix products, arithmetic and copies ran while one was open for 7% of the time, Pallas kernels for 0%

profile of v1, /device:TPU:2, one launch (start us, length us, event | category | flops | bytes accessed | tf_op | source)
XLA Modules:
  0.0 83.7 jit_solution(18371884243604729199)
XLA Ops:
  0.0 1.9 %collective-permute-start.2 = (bf16[5,160,640]{2,1,0:T(8,128)(2,1)}, bf16[5,160,640]{2,1,0:T(8,128)(2,1)S(1)}, u32[]{:S(2)}, u32[]{:S(2)}) collective-permute-start(bf16[5,160,640]{2,1,0:T(8,128)(2,1)} %param.7), channel_id=1, source_target_pairs={{0,1},{1,0},{2,3},{3,2},{4,5},{5,4},{6,7},{7,6},{8,9},{9,8},{10,11... | collective-permute-start | bytes 3072008 | tf_op jit(solution)/shard_map/ppermute | solution.py:261
  1.9 0.9 %fusion.11 = (bf16[5,1,640]{2,1,0:T(2,128)(2,1)S(1)}, bf16[5,1,640]{2,1,0:T(2,128)(2,1)S(1)}) fusion(bf16[5,160,640]{2,1,0:T(8,128)(2,1)} %param.7), kind=kLoop, calls=%fused_computation.36 | loop fusion | bytes 25600 | tf_op jit(solution)/shard_map/slice | solution.py:259
  2.8 1.3 %collective-permute-start.3 = (bf16[5,640]{1,0:T(8,128)(2,1)S(1)}, bf16[5,640]{1,0:T(8,128)(2,1)S(1)}, u32[]{:S(2)}, u32[]{:S(2)}) collective-permute-start(bf16[5,640]{1,0:T(8,128)(2,1)S(1)} %fusion.5), channel_id=1, source_target_pairs={{2,0},{1,3},{6,4},{5,7},{10,8},{9,11},{14,12},{13,15},{18,16},{17,... | collective-permute-start | bytes 19208 | tf_op jit(solution)/shard_map/ppermute | solution.py:260
  4.1 0.7 collective-permute-start.4
  4.8 9.2 %collective-permute-start.1 = (bf16[5,8,2,640]{3,2,1,0:T(2,128)(2,1)}, bf16[5,8,2,640]{3,2,1,0:T(2,128)(2,1)S(1)}, u32[]{:S(2)}, u32[]{:S(2)}) collective-permute-start(bf16[5,8,2,640]{3,2,1,0:T(2,128)(2,1)} %param.6), channel_id=1, source_target_pairs={{0,2},{2,0},{1,3},{3,1},{4,6},{6,4},{5,7},{7,5},{8,10},{10,8},{9,1... | collective-permute-start | bytes 307208 | tf_op jit(solution)/shard_map/ppermute | solution.py:263
  14.0 1.9 %collective-permute-start = (bf16[5,8,2,640]{3,2,1,0:T(2,128)(2,1)}, bf16[5,8,2,640]{3,2,1,0:T(2,128)(2,1)S(1)}, u32[]{:S(2)}, u32[]{:S(2)}) collective-permute-start(bf16[5,8,2,640]{3,2,1,0:T(2,128)(2,1)} %param.5), channel_id=1, source_target_pairs={{0,2},{2,0},{1,3},{3,1},{4,6},{6,4},{5,7},{7,5},{8,10},{10,8},{9,1... | collective-permute-start | bytes 307208 | tf_op jit(solution)/shard_map/ppermute | solution.py:262
  16.0 0.8 sine_bitcast_fusion
  16.8 0.1 compare_convert_fusion
  16.9 0.1 compare_select_fusion.2
  17.1 0.7 convert_element_type.33
  17.8 0.1 broadcast_in_dim.11
  17.9 0.2 broadcast_in_dim.12
  18.2 4.1 %collective-permute-done = bf16[5,8,2,640]{3,2,1,0:T(2,128)(2,1)S(1)} collective-permute-done((bf16[5,8,2,640]{3,2,1,0:T(2,128)(2,1)}, bf16[5,8,2,640]{3,2,1,0:T(2,128)(2,1)S(1)}, u32[]{:S(2)}, u32[]{:S(2)}) %collective-permute-start) | collective-permute-done | bytes 102432 | tf_op jit(solution)/shard_map/ppermute | solution.py:262
  22.3 1.0 %broadcast_select_fusion.3 = (bf16[5,2,8,640]{3,2,1,0:T(8,128)(2,1)S(1)}, bf16[5,2,8,640]{3,2,1,0:T(8,128)(2,1)S(1)}, bf16[5,2,8,640]{3,2,1,0:T(8,128)(2,1)S(1)}, bf16[5,2,8,640]{3,2,1,0:T(8,128)(2,1)S(1)}) fusion(bf16[5,2,8,640]{3,2,1,0:T(8,128)(2,1)} %bitcast.24, bf16[5,2,8,640]{3,2,1,0:T(8,128)(2,1)S(1)} %bitcast.26, pred[]{:T(512)S(6)} %eq.11, ...), kind=kLoop, calls=%fused_computation.11 | loop fusion | flops 204800 | bytes 819201 | tf_op jit(solution)/shard_map/jit(_where)/select_n | solution.py:272
  23.3 0.3 pad_maximum_fusion.2
  23.6 0.1 stack.30
  23.7 0.4 slice_maximum_fusion
  24.0 0.5 pad_maximum_fusion.3
  24.6 0.2 broadcast_multiply_fusion
  24.9 0.2 broadcast_select_fusion.1
  25.1 0.2 pad_maximum_fusion.basis_ref
  25.4 0.2 broadcast_in_dim.14.row_waves_ref
  25.6 57.3 %shard_map.46 = f32[5,16,640]{2,1,0:T(8,128)S(1)} custom-call(s32[5]{0:T(128)S(1)} %get-tuple-element.6.waves_ref, f32[2,5]{1,0:T(2,128)S(1)} %pad_maximum_fusion.5.factors_ref, bf16[5,128,640]{2,1,0:T(8,128)(2,1)S(1)} %bitcast.19, bf16[5,384,640]{2,1,0:T(8,128)(2,1)S(1)} %pad_maximum_fusion.basis_ref, f32[8,1280]{1,0:T(8,128)S(1)} %broadcast_in_dim.13.lane_waves_ref, ...), custom_call_target="tpu_custom_call" | custom-call | tf_op jit(solution)/shard_map/pallas_call | solution.py:295
  82.9 0.8 reshape.137
  (14 shorter events, 0.2 us)
Async XLA Ops:
  0.0 24.9 %collective-permute-start.2 = (bf16[5,160,640]{2,1,0:T(8,128)(2,1)}, bf16[5,160,640]{2,1,0:T(8,128)(2,1)S(1)}, u32[]{:S(2)}, u32[]{:S(2)}) collective-permute-start(bf16[5,160,640]{2,1,0:T(8,128)(2,1)} %param.7), channel_id=1, source_target_pairs={{0,1},{1,0},{2,3},{3,2},{4,5},{5,4},{6,7},{7,6},{8,9},{9,8},{10,11... | collective-permute-start | bytes 3072008 | tf_op jit(solution)/shard_map/ppermute | solution.py:261
  2.8 15.3 %collective-permute-start.3 = (bf16[5,640]{1,0:T(8,128)(2,1)S(1)}, bf16[5,640]{1,0:T(8,128)(2,1)S(1)}, u32[]{:S(2)}, u32[]{:S(2)}) collective-permute-start(bf16[5,640]{1,0:T(8,128)(2,1)S(1)} %fusion.5), channel_id=1, source_target_pairs={{2,0},{1,3},{6,4},{5,7},{10,8},{9,11},{14,12},{13,15},{18,16},{17,... | collective-permute-start | bytes 19208 | tf_op jit(solution)/shard_map/ppermute | solution.py:260
  4.1 14.0 %collective-permute-start.4 = (bf16[5,640]{1,0:T(8,128)(2,1)S(1)}, bf16[5,640]{1,0:T(8,128)(2,1)S(1)}, u32[]{:S(2)}, u32[]{:S(2)}) collective-permute-start(bf16[5,640]{1,0:T(8,128)(2,1)S(1)} %fusion.5), channel_id=1, source_target_pairs={{2,1},{1,2},{6,5},{5,6},{10,9},{9,10},{14,13},{13,14},{18,17},{17,... | collective-permute-start | bytes 19208 | tf_op jit(solution)/shard_map/ppermute | solution.py:260
  4.8 13.4 %collective-permute-start.1 = (bf16[5,8,2,640]{3,2,1,0:T(2,128)(2,1)}, bf16[5,8,2,640]{3,2,1,0:T(2,128)(2,1)S(1)}, u32[]{:S(2)}, u32[]{:S(2)}) collective-permute-start(bf16[5,8,2,640]{3,2,1,0:T(2,128)(2,1)} %param.6), channel_id=1, source_target_pairs={{0,2},{2,0},{1,3},{3,1},{4,6},{6,4},{5,7},{7,5},{8,10},{10,8},{9,1... | collective-permute-start | bytes 307208 | tf_op jit(solution)/shard_map/ppermute | solution.py:263
  14.0 8.3 %collective-permute-start = (bf16[5,8,2,640]{3,2,1,0:T(2,128)(2,1)}, bf16[5,8,2,640]{3,2,1,0:T(2,128)(2,1)S(1)}, u32[]{:S(2)}, u32[]{:S(2)}) collective-permute-start(bf16[5,8,2,640]{3,2,1,0:T(2,128)(2,1)} %param.5), channel_id=1, source_target_pairs={{0,2},{2,0},{1,3},{3,1},{4,6},{6,4},{5,7},{7,5},{8,10},{10,8},{9,1... | collective-permute-start | bytes 307208 | tf_op jit(solution)/shard_map/ppermute | solution.py:262
  17.9 6.9 %copy-start = (bf16[5,160,640]{2,1,0:T(8,128)(2,1)S(1)}, bf16[5,160,640]{2,1,0:T(8,128)(2,1)}, u32[]{:S(2)}) copy-start(bf16[5,160,640]{2,1,0:T(8,128)(2,1)} %param.7) | copy-start | bytes 3072004

commit v2 on v1

v2 whole, which is shorter than its diff:
```python
import functools
import math

import jax
import jax.numpy as jnp
from jax import lax
from jax.experimental import pallas as pl
from jax.experimental.pallas import tpu as pltpu
from jax.sharding import PartitionSpec as P

LON = 2560
SLOTS = 5
BLOCKS = 5
LANES = 128
GROUP = 16
HALF_LEVELS = 8
ROWS = 16


def cos_sin(turns):
    x = turns - jnp.floor(turns + 0.5)
    u = x * x
    cos = jnp.full_like(u, (2 * math.pi) ** 18 / math.factorial(18) * -1.0)
    sin = jnp.full_like(u, (2 * math.pi) ** 19 / math.factorial(19) * -1.0)
    for i in range(8, -1, -1):
        sign = 1.0 if i % 2 == 0 else -1.0
        cos = cos * u + sign * (2 * math.pi) ** (2 * i) / math.factorial(2 * i)
        sin = sin * u + sign * (2 * math.pi) ** (2 * i + 1) / math.factorial(2 * i + 1)
    return cos, sin * x


def tile_rows(value, count):
    return jnp.concatenate([value] * count, axis=0)


def kernel(
    n_lat, half_rows, degrees,
    assign_ref, u_ref, v_ref, basis_ref, lane_waves_ref,
    out_ref,
    wide_basis, u_other, v_other, edge_send, edge_recv,
    send, recv, coeffs, flux, back, ret, sum_send, sum_recv, table_q, table_k, row_waves,
    ready, load_sem, swap_send_sem, swap_recv_sem, edge_send_sem, edge_recv_sem,
    send_sem, recv_sem, local_sem, back_send_sem, back_recv_sem, back_local_sem, sum_send_sem, sum_recv_sem,
):
    me = lax.axis_index("lat")
    lev = lax.axis_index("lev")
    x_hi = lev // 2
    core = lax.rem(lev, 2)
    spread = 2 * lev
    rows_x = 2 * half_rows
    wide = wide_basis.shape[1]
    total = SLOTS * n_lat * 2
    units = BLOCKS * GROUP
    mesh_id = pl.DeviceIdType.MESH

    my_group = me // 8
    my_z = lax.rem(lax.rem(me, 8) + 32 - lax.rem(my_group * 3 + spread, 8), 8)
    my_block = (5 * my_z + 7) // 8
    active = (8 * my_block) // 5 == my_z
    my_level = my_group // 2
    my_half = lax.rem(my_group + my_level, 2)

    def owner_of(block, half, level):
        group = level * 2 + lax.rem(level + half, 2)
        return group * 8 + lax.rem((8 * block) // 5 + lax.rem(group * 3 + spread, 8), 8)

    own_rows = pl.ds(pl.multiple_of(core * half_rows, ROWS), half_rows)
    load = pltpu.make_async_copy(basis_ref, wide_basis.at[:, own_rows], load_sem)
    load.start()

    barrier = pltpu.get_barrier_semaphore()
    for i in range(1, 4):
        pl.semaphore_signal(barrier, inc=1, device_id={"lev": lax.rem(lev + i, 4)}, device_id_type=mesh_id)
    plane = me - lax.rem(me, GROUP)

    @pl.loop(1, GROUP)
    def _(i):
        peer = plane + lax.rem(me + i, GROUP)
        pl.semaphore_signal(barrier, inc=1, device_id={"lat": peer}, device_id_type=mesh_id)

    planes = n_lat // GROUP

    @pl.loop(1, planes)
    def _(i):
        peer = lax.rem(me + i * GROUP, n_lat)
        pl.semaphore_signal(barrier, inc=1, device_id={"lat": peer}, device_id_type=mesh_id)

    pl.semaphore_wait(barrier, 3 + GROUP - 1 + planes - 1)

    partner = lax.rem(lev + 2, 4)
    sibling = 2 * x_hi + 1 - core

    def swap(i, source, target, device):
        return pltpu.make_async_remote_copy(
            src_ref=source, dst_ref=target, send_sem=swap_send_sem.at[i], recv_sem=swap_recv_sem.at[i],
            device_id={"lev": device}, device_id_type=mesh_id,
        )

    swap_u = swap(0, u_ref, u_other, partner)
    swap_v = swap(1, v_ref, v_other, partner)
    swap_u.start()
    swap_v.start()

    @pl.loop(1, planes)
    def _(i):
        peer = lax.rem(me + i * GROUP, n_lat)
        pl.semaphore_signal(ready, inc=1, device_id={"lat": peer}, device_id_type=mesh_id)

    load.wait()
    swap_basis = swap(2, wide_basis.at[:, own_rows], wide_basis.at[:, own_rows], sibling)
    swap_basis.start()

    inner = x_hi + core == 1
    edge_base = 2 - 2 * x_hi

    def edge_copy(i):
        return pltpu.make_async_remote_copy(
            src_ref=edge_send, dst_ref=edge_recv, send_sem=edge_send_sem.at[i], recv_sem=edge_recv_sem,
            device_id={"lev": edge_base + i}, device_id_type=mesh_id,
        )

    @pl.when(inner & (x_hi == 1))
    def _():
        for k in range(SLOTS):
            edge_send[k] = jnp.broadcast_to(wide_basis[k, 0:ROWS, :][0:1], (2, degrees))

    @pl.when(inner & (x_hi == 0))
    def _():
        for k in range(SLOTS):
            edge_send[k] = jnp.broadcast_to(wide_basis[k, rows_x - ROWS : rows_x, :][ROWS - 1 :], (2, degrees))

    @pl.when(inner)
    def _():
        edge_copy(0).start()
        edge_copy(1).start()

    for t in range(total // LANES):
        square = jnp.broadcast_to(lane_waves_ref[0:1, t * LANES : (t + 1) * LANES], (LANES, LANES))
        row_waves[t * LANES : (t + 1) * LANES, :] = square.T

    edge_copy(0).wait_recv()
    for k in range(SLOTS):
        wide_basis[k, rows_x:wide, :] = jnp.broadcast_to(edge_recv[k][0:1], (wide - rows_x, degrees))
    swap_basis.wait()

    send_rows = send.reshape(2, BLOCKS, SLOTS, 2, ROWS, LANES)
    lane = lax.broadcasted_iota(jnp.int32, (2 * ROWS, wide), 1)
    row = lax.broadcasted_iota(jnp.int32, (2 * ROWS, wide), 0)
    half_sign = jnp.where(row < ROWS, -0.5, 0.5)
    even = lax.rem(row, 2) == 0
    lane_tile = lax.broadcasted_iota(jnp.int32, (ROWS, LANES), 1)
    degree = lax.broadcasted_iota(jnp.int32, (8, degrees), 1)
    degree_sign = (1 - 2 * lax.rem(degree, 2)).astype(jnp.float32)

    def factors(k):
        wave = assign_ref[me * SLOTS + k]
        parity = (1 - 2 * lax.rem(wave, 2)).astype(jnp.float32)
        live = jnp.where(degree >= wave, 1.0, 0.0)
        return wave, parity, live, live * (parity * degree_sign)

    def meridional(half, u_rows, v_rows):
        @pl.loop(0, SLOTS)
        def _(k):
            wave, parity, live, signed = factors(k)
            live = tile_rows(live, 2).astype(jnp.bfloat16)
            signed = tile_rows(signed, 2).astype(jnp.bfloat16)
            u, v = u_rows[k], v_rows[k]
            lhs = jnp.concatenate([u * live, u * signed, v * live, v * signed], axis=0)
            fields = lax.dot_general(
                lhs, wide_basis[k], (((1,), (1,)), ((), ())), preferred_element_type=jnp.float32
            )
            wind, other = fields[: 2 * ROWS], fields[2 * ROWS :]
            turned = jnp.where(even, pltpu.roll(other, 2 * ROWS - 1, 0), -pltpu.roll(other, 1, 0))
            sine = cos_sin(jnp.full((8, wide), 1.0 / LON, jnp.float32) * wave.astype(jnp.float32))[1]
            before = pltpu.roll(wind, 1, 1)
            after = pltpu.roll(wind, wide - 1, 1)
            swapped = jnp.concatenate([wind[ROWS:], wind[:ROWS]], axis=0)
            before = jnp.where((lane == 0) & (x_hi == 0), -parity * wind, before)
            after = jnp.where((lane == rows_x - 1) & (x_hi == 1), swapped, after)
            curl = tile_rows(sine, 2 * ROWS // 8) * turned + half_sign * (before - after)
            for f, value in enumerate((wind, curl)):
                north, south = value[:ROWS], value[ROWS:]
                tail = 2 * LANES
                mixed = jnp.where(
                    lane_tile < LANES // 2,
                    north[:, tail : tail + LANES],
                    pltpu.roll(south[:, tail : tail + LANES], LANES // 2, 1),
                )
                tiles = (north[:, :LANES], north[:, LANES:tail], south[:, :LANES], south[:, LANES:tail], mixed)
                for b, tile in enumerate(tiles):
                    send_rows[f, b, k, half] = tile.astype(jnp.bfloat16)

        @pl.loop(0, units // 2)
        def _(i):
            block = lax.rem(i, BLOCKS)
            level = lax.rem(i // BLOCKS + my_level, HALF_LEVELS)
            source = send.at[:, block, :, half, level]
            owner = owner_of(block, half, level)

            @pl.when(owner != me)
            def _():
                pltpu.make_async_remote_copy(
                    src_ref=source, dst_ref=recv.at[:, me], send_sem=send_sem, recv_sem=recv_sem,
                    device_id={"lat": owner}, device_id_type=mesh_id,
                ).start()

            @pl.when(owner == me)
            def _():
                pltpu.make_async_copy(source, recv.at[:, me], local_sem).start()

    pl.semaphore_wait(ready, planes - 1)
    meridional(0, u_ref.reshape(SLOTS, ROWS, degrees), v_ref.reshape(SLOTS, ROWS, degrees))

    chunk = 64

    @pl.loop(0, total // chunk)
    def _(i):
        rows = pl.ds(pl.multiple_of(i * chunk, chunk), chunk)
        wave = row_waves[rows, :]
        column = lax.broadcasted_iota(jnp.int32, (chunk, LANES), 1).astype(jnp.float32)
        part = lax.broadcasted_iota(jnp.int32, (chunk, LANES), 0)
        shift = lax.rem(part, 2).astype(jnp.float32) * 0.25
        cos, sin = cos_sin(wave * column * (1.0 / LON) - shift)
        turn_cos, turn_sin = cos_sin(wave * (LANES / LON))
        for step in range(LON // LANES):
            table_k[rows, step * LANES : (step + 1) * LANES] = cos.astype(jnp.bfloat16)
            cos, sin = cos * turn_cos - sin * turn_sin, sin * turn_cos + cos * turn_sin

    swap_u.wait()
    swap_v.wait()
    meridional(1, u_other.reshape(SLOTS, ROWS, degrees), v_other.reshape(SLOTS, ROWS, degrees))

    width = total // 2
    for part in range(2):
        lanes = pl.ds(part * width, width)
        height = 16
        wave = jnp.broadcast_to(lane_waves_ref[0:1, lanes], (height, width))
        position = lax.broadcasted_iota(jnp.int32, (height, width), 0).astype(jnp.float32)
        side = lax.broadcasted_iota(jnp.int32, (height, width), 1)
        shift = lax.rem(side, 2).astype(jnp.float32) * 0.25
        start = cos_sin(wave * position * (1.0 / LON) - shift)
        turn_cos, turn_sin = cos_sin(lane_waves_ref[0:8, lanes] * (height / LON))
        turn_cos, turn_sin = tile_rows(turn_cos, 2), tile_rows(turn_sin, 2)

        def advance(i, carry):
            cos, sin = carry
            table_q[pl.ds(pl.multiple_of(i * height, height), height), lanes] = cos.astype(jnp.bfloat16)
            return cos * turn_cos - sin * turn_sin, sin * turn_cos + cos * turn_sin

        lax.fori_loop(0, LON // height, advance, start)

    @pl.when(inner)
    def _():
        edge_copy(0).wait_send()
        edge_copy(1).wait_send()

    @pl.when(active)
    def _():
        remote = recv.at[:, pl.ds(0, n_lat - 1)]
        pltpu.make_async_copy(remote, remote, recv_sem).wait()
        pltpu.make_async_copy(recv.at[:, 0], recv.at[:, 0], local_sem).wait()
        recv_rows = recv.reshape(2, total, LANES)
        coeffs[:, :LANES] = recv_rows[0]
        coeffs[:, LANES:] = recv_rows[1]
        step = 256

        @pl.loop(0, LON // step)
        def _(i):
            rows = pl.ds(pl.multiple_of(i * step, step), step)
            grid = jnp.dot(table_q[rows, :], coeffs[...], preferred_element_type=jnp.float32)
            flux[rows, :] = (grid[:, :LANES] * grid[:, LANES:]).astype(jnp.bfloat16)

        back_rows = back.reshape(total, LANES)
        pieces = 4
        owners = n_lat // pieces
        high = total // pieces

        @pl.loop(0, pieces)
        def _(i):
            piece = lax.rem(i + me // owners, pieces)
            rows = pl.ds(pl.multiple_of(piece * high, high), high)
            zonal = jnp.dot(table_k[rows, :], flux[...], preferred_element_type=jnp.float32)
            back_rows[rows, :] = (zonal * (1.0 / math.sqrt(LON))).astype(jnp.bfloat16)

            @pl.loop(0, owners)
            def _(j):
                owner = piece * owners + lax.rem(j + me, owners)
                target = ret.at[my_block, :, my_half, my_level]

                @pl.when(owner != me)
                def _():
                    pltpu.make_async_remote_copy(
                        src_ref=back.at[owner], dst_ref=target, send_sem=back_send_sem, recv_sem=back_recv_sem,
                        device_id={"lat": owner}, device_id_type=mesh_id,
                    ).start()

                @pl.when(owner == me)
                def _():
                    pltpu.make_async_copy(back.at[owner], target, back_local_sem).start()

        pltpu.make_async_copy(back.at[me], back.at[me], back_local_sem).wait()
        sent = recv.at[:, pl.ds(0, units - 1)]
        pltpu.make_async_copy(sent, sent, send_sem).wait()
        got = recv.at[0, pl.ds(0, units - 1)]
        pltpu.make_async_copy(got, got, back_recv_sem).wait()

    @pl.when(jnp.logical_not(active))
    def _():
        sent = recv.at[:, pl.ds(0, units)]
        pltpu.make_async_copy(sent, sent, send_sem).wait()
        got = recv.at[0, pl.ds(0, units)]
        pltpu.make_async_copy(got, got, back_recv_sem).wait()

    ret_rows = ret.reshape(BLOCKS, SLOTS, 2 * ROWS, LANES)
    wide_lane = lax.broadcasted_iota(jnp.int32, (2 * ROWS, LANES), 1)

    def sum_copy(k):
        return pltpu.make_async_remote_copy(
            src_ref=sum_send.at[k], dst_ref=sum_recv.at[k],
            send_sem=sum_send_sem.at[k], recv_sem=sum_recv_sem.at[k],
            device_id={"lev": partner}, device_id_type=mesh_id,
        )

    @pl.loop(0, SLOTS)
    def _(k):
        wave, parity, live, signed = factors(k)
        mixed = ret_rows[4, k].astype(jnp.float32)
        zero = jnp.zeros_like(mixed)
        tail_north = jnp.where(wide_lane < LANES // 2, mixed, zero).astype(jnp.bfloat16)
        tail_south = jnp.where(wide_lane < LANES // 2, pltpu.roll(mixed, LANES // 2, 1), zero).astype(jnp.bfloat16)
        north = jnp.concatenate([ret_rows[0, k], ret_rows[1, k], tail_north], axis=1)
        south = jnp.concatenate([ret_rows[2, k], ret_rows[3, k], tail_south], axis=1)
        both = jnp.dot(
            jnp.concatenate([north, south], axis=0), wide_basis[k], preferred_element_type=jnp.float32
        )
        combined = tile_rows(live, 4) * both[: 2 * ROWS] + tile_rows(signed, 4) * both[2 * ROWS :]
        sum_send[k] = combined[ROWS:].astype(jnp.bfloat16)
        sum_copy(k).start()
        out_ref[k] = combined[:ROWS]

    @pl.when(active)
    def _():
        sent = recv.at[0, pl.ds(0, n_lat - 1)]
        pltpu.make_async_copy(sent, sent, back_send_sem).wait()

    @pl.loop(0, SLOTS)
    def _(k):
        sum_copy(k).wait()
        out_ref[k] += sum_recv[k].astype(jnp.float32)


def body(n_lat, assign, u_spec, v_spec, basis):
    slots, lev_dev, _, degrees = u_spec.shape
    half_rows = basis.shape[1]
    order = jnp.repeat(assign.astype(jnp.float32), 2)
    total = order.shape[0]
    lane_waves = jnp.broadcast_to(order[None, :], (8, total))
    wide = 3 * LANES

    vmem = pl.BlockSpec(memory_space=pltpu.VMEM)
    smem = pl.BlockSpec(memory_space=pltpu.SMEM)
    bf16 = jnp.bfloat16
    dma = pltpu.SemaphoreType.DMA
    result = pl.pallas_call(
        functools.partial(kernel, n_lat, half_rows, degrees),
        out_shape=jax.ShapeDtypeStruct((slots, ROWS, degrees), jnp.float32),
        in_specs=[smem, vmem, vmem, pl.BlockSpec(memory_space=pl.ANY), vmem],
        out_specs=vmem,
        scratch_shapes=[
            pltpu.VMEM((slots, wide, degrees), bf16),
            pltpu.VMEM((slots, lev_dev, 2, degrees), bf16),
            pltpu.VMEM((slots, lev_dev, 2, degrees), bf16),
            pltpu.VMEM((slots, 2, degrees), bf16),
            pltpu.VMEM((slots, 2, degrees), bf16),
            pltpu.VMEM((2, BLOCKS, SLOTS, 2, HALF_LEVELS, 2, LANES), bf16),
            pltpu.VMEM((2, n_lat, SLOTS, 2, LANES), bf16),
            pltpu.VMEM((total, 2 * LANES), bf16),
            pltpu.VMEM((LON, LANES), bf16),
            pltpu.VMEM((n_lat, SLOTS, 2, LANES), bf16),
            pltpu.VMEM((BLOCKS, SLOTS, 2, HALF_LEVELS, 2, LANES), bf16),
            pltpu.VMEM((SLOTS, ROWS, degrees), bf16),
            pltpu.VMEM((SLOTS, ROWS, degrees), bf16),
            pltpu.VMEM((LON, total), bf16),
            pltpu.VMEM((total, LON), bf16),
            pltpu.VMEM((total, LANES), jnp.float32),
            pltpu.SemaphoreType.REGULAR,
            dma, dma((3,)), dma((3,)), dma((2,)), dma,
            dma, dma, dma, dma, dma, dma, dma((SLOTS,)), dma((SLOTS,)),
        ],
        compiler_params=pltpu.CompilerParams(
            collective_id=0, has_side_effects=True, vmem_limit_bytes=48 * 1024 * 1024
        ),
    )(assign, u_spec, v_spec, basis, lane_waves)
    return result.reshape(slots, lev_dev, 2, degrees)


def solution(mesh):
    return jax.shard_map(
        functools.partial(body, mesh.shape["lat"]),
        mesh=mesh,
        in_specs=(
            P(),
            P("lat", "lev", None, None),
            P("lat", "lev", None, None),
            P("lat", "lev", None),
        ),
        out_specs=P("lat", "lev", None, None),
        check_vma=False,
    )
```

time: 84.1 us -> 68.1 us (0.81)
  the two profiles are of different devices: /device:TPU:2 before, /device:TPU:6 now
where the time goes in v2:
time: 68.1 us; the launch traced here: 67.9 us
  Pallas kernels  64 us (94%)
  local copies, waits for them, and re-layouts  3.07 us (5%)
  other arithmetic  0.69 us (1%)
    pallas_call x1, Pallas kernels, body(): pl.pallas_call(functools.partial(kernel, n_lat, half_rows, degrees), out_...  64 us
    unnamed x8, local copies, waits for them, and re-layouts  1.93 us

profile of v2, /device:TPU:6, one launch (start us, length us, event | category | flops | bytes accessed | tf_op | source)
XLA Modules:
  0.0 67.9 jit_solution(4109978108300696879)
XLA Ops:
  0.0 0.7 %convert_element_type.3 = f32[640]{0:T(1024)S(1)} convert(s32[640]{0:T(1024)} %assign_ref.1) | non-fusion elementwise | flops 640 | bytes 5120 | tf_op jit(solution)/shard_map/convert_element_type | solution.py:355
  0.7 0.1 broadcast_in_dim.10
  0.8 0.0 copy-start.1
  0.8 0.0 copy-start.2
  0.9 0.2 broadcast_in_dim.11
  1.1 0.0 copy-start.3
  1.1 0.6 copy-done.1
  1.7 0.1 copy-done.2
  1.8 0.0 copy-done.3
  1.8 0.0 copy-start
  1.8 1.2 %copy-done = bf16[5,160,640]{2,1,0:T(8,128)(2,1)S(1)} copy-done((bf16[5,160,640]{2,1,0:T(8,128)(2,1)S(1)}, bf16[5,160,640]{2,1,0:T(8,128)(2,1)}, u32[]{:S(2)}) %copy-start) | copy-done | bytes 1024024
  3.0 64.0 %shard_map.46 = f32[5,16,640]{2,1,0:T(8,128)S(1)} custom-call(s32[640]{0:T(1024)S(1)} %copy-done.3, bf16[5,8,2,640]{3,2,1,0:T(2,128)(2,1)S(1)} %copy-done.1, bf16[5,8,2,640]{3,2,1,0:T(2,128)(2,1)S(1)} %copy-done.2, bf16[5,160,640]{2,1,0:T(8,128)(2,1)S(1)} %copy-done, f32[8,1280]{1,0:T(8,128)S(1)} %broadcast_in_dim.12.lane_waves_ref), custom_call_target="tpu_custom_call" | custom-call | tf_op jit(solution)/shard_map/pallas_call | solution.py:364
  67.1 0.8 %reshape.4 = f32[5,8,2,640]{3,2,1,0:T(2,128)} reshape(f32[5,16,640]{2,1,0:T(8,128)S(1)} %shard_map.46) | data formatting | bytes 409600 | tf_op jit(solution)/shard_map/reshape | solution.py:394
  (1 shorter events, 0.0 us)
Async XLA Ops:
  0.8 0.9 %copy-start.1 = (bf16[5,8,2,640]{3,2,1,0:T(2,128)(2,1)S(1)}, bf16[5,8,2,640]{3,2,1,0:T(2,128)(2,1)}, u32[]{:S(2)}) copy-start(bf16[5,8,2,640]{3,2,1,0:T(2,128)(2,1)} %u_ref.1) | copy-start | bytes 307204
  0.8 0.9 %copy-start.2 = (bf16[5,8,2,640]{3,2,1,0:T(2,128)(2,1)S(1)}, bf16[5,8,2,640]{3,2,1,0:T(2,128)(2,1)}, u32[]{:S(2)}) copy-start(bf16[5,8,2,640]{3,2,1,0:T(2,128)(2,1)} %v_ref.1) | copy-start | bytes 307204
  1.1 0.7 %copy-start.3 = (s32[640]{0:T(1024)S(1)}, s32[640]{0:T(1024)}, u32[]{:S(2)}) copy-start(s32[640]{0:T(1024)} %assign_ref.1) | copy-start | bytes 7684
  1.8 1.2 %copy-start = (bf16[5,160,640]{2,1,0:T(8,128)(2,1)S(1)}, bf16[5,160,640]{2,1,0:T(8,128)(2,1)}, u32[]{:S(2)}) copy-start(bf16[5,160,640]{2,1,0:T(8,128)(2,1)} %basis_ref.1) | copy-start | bytes 3072004

commit v3 on v2

--- a/solution.py
+++ b/solution.py
@@ -33,12 +33,17 @@
     return jnp.concatenate([value] * count, axis=0)
 
 
+def parity_of(wave):
+    return 1.0 - 2.0 * (wave - 2.0 * jnp.floor(0.5 * wave))
+
+
 def kernel(
     n_lat, half_rows, degrees,
-    assign_ref, u_ref, v_ref, basis_ref, lane_waves_ref,
+    assign_ref, assign_lanes_ref, u_ref, v_ref, basis_ref,
     out_ref,
-    wide_basis, u_other, v_other, edge_send, edge_recv,
-    send, recv, coeffs, flux, back, ret, sum_send, sum_recv, table_q, table_k, row_waves,
+    wide_basis, u_own, v_own, u_other, v_other, edge_send, edge_recv,
+    send, recv, split, cos_coeffs, sin_coeffs, cos_flux, sin_flux, mix, back, ret, sum_send, sum_recv,
+    cos_q, sin_q, end_q, cos_k, sin_k, row_waves,
     ready, load_sem, swap_send_sem, swap_recv_sem, edge_send_sem, edge_recv_sem,
     send_sem, recv_sem, local_sem, back_send_sem, back_recv_sem, back_local_sem, sum_send_sem, sum_recv_sem,
 ):
@@ -49,7 +54,8 @@
     spread = 2 * lev
     rows_x = 2 * half_rows
     wide = wide_basis.shape[1]
-    total = SLOTS * n_lat * 2
+    waves = SLOTS * n_lat
+    half_lon = LON // 2
     units = BLOCKS * GROUP
     mesh_id = pl.DeviceIdType.MESH
 
@@ -60,13 +66,14 @@
     my_level = my_group // 2
     my_half = lax.rem(my_group + my_level, 2)
 
-    def owner_of(block, half, level):
-        group = level * 2 + lax.rem(level + half, 2)
-        return group * 8 + lax.rem((8 * block) // 5 + lax.rem(group * 3 + spread, 8), 8)
-
     own_rows = pl.ds(pl.multiple_of(core * half_rows, ROWS), half_rows)
-    load = pltpu.make_async_copy(basis_ref, wide_basis.at[:, own_rows], load_sem)
-    load.start()
+    loads = [
+        pltpu.make_async_copy(basis_ref, wide_basis.at[:, own_rows], load_sem.at[0]),
+        pltpu.make_async_copy(u_ref, u_own, load_sem.at[1]),
+        pltpu.make_async_copy(v_ref, v_own, load_sem.at[2]),
+    ]
+    for load in loads:
+        load.start()
 
     barrier = pltpu.get_barrier_semaphore()
     for i in range(1, 4):
@@ -96,18 +103,16 @@
             device_id={"lev": device}, device_id_type=mesh_id,
         )
 
-    swap_u = swap(0, u_ref, u_other, partner)
-    swap_v = swap(1, v_ref, v_other, partner)
-    swap_u.start()
-    swap_v.start()
+    swap_u = swap(0, u_own, u_other, partner)
+    swap_v = swap(1, v_own, v_other, partner)
+    swap_basis = swap(2, wide_basis.at[:, own_rows], wide_basis.at[:, own_rows], sibling)
 
     @pl.loop(1, planes)
     def _(i):
         peer = lax.rem(me + i * GROUP, n_lat)
         pl.semaphore_signal(ready, inc=1, device_id={"lat": peer}, device_id_type=mesh_id)
 
-    load.wait()
-    swap_basis = swap(2, wide_basis.at[:, own_rows], wide_basis.at[:, own_rows], sibling)
+    loads[0].wait()
     swap_basis.start()
 
     inner = x_hi + core == 1
@@ -134,9 +139,31 @@
         edge_copy(0).start()
         edge_copy(1).start()
 
-    for t in range(total // LANES):
-        square = jnp.broadcast_to(lane_waves_ref[0:1, t * LANES : (t + 1) * LANES], (LANES, LANES))
-        row_waves[t * LANES : (t + 1) * LANES, :] = square.T
+    loads[1].wait()
+    swap_u.start()
+    loads[2].wait()
+    swap_v.start()
+
+    lane_waves = []
+    for t in range(waves // LANES):
+        line = assign_lanes_ref[t : t + 1, :].astype(jnp.float32)
+        lane_waves.append(jnp.broadcast_to(line, (8, LANES)))
+        row_waves[t * LANES : (t + 1) * LANES, :] = jnp.broadcast_to(line, (LANES, LANES)).T
+
+    chunk = 64
+
+    @pl.loop(0, waves // chunk)
+    def _(i):
+        rows = pl.ds(pl.multiple_of(i * chunk, chunk), chunk)
+        wave = row_waves[rows, :]
+        column = lax.broadcasted_iota(jnp.int32, (chunk, LANES), 1).astype(jnp.float32)
+        cos, sin = cos_sin(wave * column * (1.0 / LON))
+        turn_cos, turn_sin = cos_sin(wave * (LANES / LON))
+        for step in range(half_lon // LANES):
+            lanes = slice(step * LANES, (step + 1) * LANES)
+            cos_k[rows, lanes] = cos.astype(jnp.bfloat16)
+            sin_k[rows, lanes] = sin.astype(jnp.bfloat16)
+            cos, sin = cos * turn_cos - sin * turn_sin, sin * turn_cos + cos * turn_sin
 
     edge_copy(0).wait_recv()
     for k in range(SLOTS):
@@ -159,16 +186,15 @@
         return wave, parity, live, live * (parity * degree_sign)
 
     def meridional(half, u_rows, v_rows):
-        @pl.loop(0, SLOTS)
-        def _(k):
+        for k in range(SLOTS):
             wave, parity, live, signed = factors(k)
             live = tile_rows(live, 2).astype(jnp.bfloat16)
             signed = tile_rows(signed, 2).astype(jnp.bfloat16)
             u, v = u_rows[k], v_rows[k]
             lhs = jnp.concatenate([u * live, u * signed, v * live, v * signed], axis=0)
             fields = lax.dot_general(
-                lhs, wide_basis[k], (((1,), (1,)), ((), ())), preferred_element_type=jnp.float32
-            )
+                wide_basis[k], lhs, (((1,), (1,)), ((), ())), preferred_element_type=jnp.float32
+            ).T
             wind, other = fields[: 2 * ROWS], fields[2 * ROWS :]
             turned = jnp.where(even, pltpu.roll(other, 2 * ROWS - 1, 0), -pltpu.roll(other, 1, 0))
             sine = cos_sin(jnp.full((8, wide), 1.0 / LON, jnp.float32) * wave.astype(jnp.float32))[1]
@@ -190,64 +216,56 @@
                 for b, tile in enumerate(tiles):
                     send_rows[f, b, k, half] = tile.astype(jnp.bfloat16)
 
-        @pl.loop(0, units // 2)
-        def _(i):
-            block = lax.rem(i, BLOCKS)
-            level = lax.rem(i // BLOCKS + my_level, HALF_LEVELS)
-            source = send.at[:, block, :, half, level]
-            owner = owner_of(block, half, level)
+        def send_unit(block, group, level, turn):
+            owner = group * 8 + lax.rem((8 * block) // 5 + turn, 8)
+            return owner, pltpu.make_async_remote_copy(
+                src_ref=send.at[:, block, :, half, level], dst_ref=recv.at[:, me], send_sem=send_sem, recv_sem=recv_sem,
+                device_id={"lat": owner}, device_id_type=mesh_id,
+            )
+
+        def place(level):
+            group = level * 2 + lax.rem(level + half, 2)
+            return group, lax.rem(group * 3 + spread, 8)
+
+        group, turn = place(my_level)
+        for block in range(BLOCKS):
+            owner, copy = send_unit(block, group, my_level, turn)
 
             @pl.when(owner != me)
             def _():
-                pltpu.make_async_remote_copy(
-                    src_ref=source, dst_ref=recv.at[:, me], send_sem=send_sem, recv_sem=recv_sem,
-                    device_id={"lat": owner}, device_id_type=mesh_id,
-                ).start()
+                copy.start()
 
             @pl.when(owner == me)
             def _():
-                pltpu.make_async_copy(source, recv.at[:, me], local_sem).start()
+                pltpu.make_async_copy(send.at[:, block, :, half, my_level], recv.at[:, me], local_sem).start()
+
+        for i in range(1, HALF_LEVELS):
+            level = lax.rem(my_level + i, HALF_LEVELS)
+            group, turn = place(level)
+            for block in range(BLOCKS):
+                send_unit(block, group, level, turn)[1].start()
 
     pl.semaphore_wait(ready, planes - 1)
-    meridional(0, u_ref.reshape(SLOTS, ROWS, degrees), v_ref.reshape(SLOTS, ROWS, degrees))
-
-    chunk = 64
-
-    @pl.loop(0, total // chunk)
-    def _(i):
-        rows = pl.ds(pl.multiple_of(i * chunk, chunk), chunk)
-        wave = row_waves[rows, :]
-        column = lax.broadcasted_iota(jnp.int32, (chunk, LANES), 1).astype(jnp.float32)
-        part = lax.broadcasted_iota(jnp.int32, (chunk, LANES), 0)
-        shift = lax.rem(part, 2).astype(jnp.float32) * 0.25
-        cos, sin = cos_sin(wave * column * (1.0 / LON) - shift)
-        turn_cos, turn_sin = cos_sin(wave * (LANES / LON))
-        for step in range(LON // LANES):
-            table_k[rows, step * LANES : (step + 1) * LANES] = cos.astype(jnp.bfloat16)
-            cos, sin = cos * turn_cos - sin * turn_sin, sin * turn_cos + cos * turn_sin
+    meridional(0, u_own.reshape(SLOTS, ROWS, degrees), v_own.reshape(SLOTS, ROWS, degrees))
 
     swap_u.wait()
     swap_v.wait()
     meridional(1, u_other.reshape(SLOTS, ROWS, degrees), v_other.reshape(SLOTS, ROWS, degrees))
 
-    width = total // 2
-    for part in range(2):
-        lanes = pl.ds(part * width, width)
-        height = 16
-        wave = jnp.broadcast_to(lane_waves_ref[0:1, lanes], (height, width))
-        position = lax.broadcasted_iota(jnp.int32, (height, width), 0).astype(jnp.float32)
-        side = lax.broadcasted_iota(jnp.int32, (height, width), 1)
-        shift = lax.rem(side, 2).astype(jnp.float32) * 0.25
-        start = cos_sin(wave * position * (1.0 / LON) - shift)
-        turn_cos, turn_sin = cos_sin(lane_waves_ref[0:8, lanes] * (height / LON))
-        turn_cos, turn_sin = tile_rows(turn_cos, 2), tile_rows(turn_sin, 2)
-
-        def advance(i, carry):
-            cos, sin = carry
-            table_q[pl.ds(pl.multiple_of(i * height, height), height), lanes] = cos.astype(jnp.bfloat16)
-            return cos * turn_cos - sin * turn_sin, sin * turn_cos + cos * turn_sin
-
-        lax.fori_loop(0, LON // height, advance, start)
+    wave = jnp.concatenate(lane_waves, axis=1)
+    end_q[...] = tile_rows(parity_of(wave), ROWS // 8).astype(jnp.bfloat16)
+    turn_cos, turn_sin = cos_sin(wave * (ROWS / LON))
+    turn_cos, turn_sin = tile_rows(turn_cos, ROWS // 8), tile_rows(turn_sin, ROWS // 8)
+    position = lax.broadcasted_iota(jnp.int32, (ROWS, waves), 0).astype(jnp.float32)
+
+    def advance(i, carry):
+        cos, sin = carry
+        rows = pl.ds(pl.multiple_of(i * ROWS, ROWS), ROWS)
+        cos_q[rows, :] = cos.astype(jnp.bfloat16)
+        sin_q[rows, :] = sin.astype(jnp.bfloat16)
+        return cos * turn_cos - sin * turn_sin, sin * turn_cos + cos * turn_sin
+
+    lax.fori_loop(0, half_lon // ROWS, advance, cos_sin(tile_rows(wave, ROWS // 8) * position * (1.0 / LON)))
 
     @pl.when(inner)
     def _():
@@ -259,44 +277,56 @@
         remote = recv.at[:, pl.ds(0, n_lat - 1)]
         pltpu.make_async_copy(remote, remote, recv_sem).wait()
         pltpu.make_async_copy(recv.at[:, 0], recv.at[:, 0], local_sem).wait()
-        recv_rows = recv.reshape(2, total, LANES)
-        coeffs[:, :LANES] = recv_rows[0]
-        coeffs[:, LANES:] = recv_rows[1]
+        recv_rows = recv.reshape(2, 2 * waves, LANES)
+        for f in range(2):
+            lanes = slice(f * LANES, (f + 1) * LANES)
+            split[f] = recv_rows[f].astype(jnp.float32)
+            cos_coeffs[:, lanes] = split[f, pl.ds(0, waves, 2), :].astype(jnp.bfloat16)
+            sin_coeffs[:, lanes] = split[f, pl.ds(1, waves, 2), :].astype(jnp.bfloat16)
         step = 256
-
-        @pl.loop(0, LON // step)
+        first_row = lax.broadcasted_iota(jnp.int32, (step, LANES), 0)
+
+        @pl.loop(0, half_lon // step)
         def _(i):
             rows = pl.ds(pl.multiple_of(i * step, step), step)
-            grid = jnp.dot(table_q[rows, :], coeffs[...], preferred_element_type=jnp.float32)
-            flux[rows, :] = (grid[:, :LANES] * grid[:, LANES:]).astype(jnp.bfloat16)
-
-        back_rows = back.reshape(total, LANES)
+            cos = jnp.dot(cos_q[rows, :], cos_coeffs[...], preferred_element_type=jnp.float32)
+            sin = jnp.dot(sin_q[rows, :], sin_coeffs[...], preferred_element_type=jnp.float32)
+            cos_u, cos_w = cos[:, :LANES], cos[:, LANES:]
+            sin_u, sin_w = sin[:, :LANES], sin[:, LANES:]
+            share = jnp.where(first_row + i * step == 0, 0.5, 1.0)
+            cos_flux[rows, :] = (share * (cos_u * cos_w + sin_u * sin_w)).astype(jnp.bfloat16)
+            sin_flux[rows, :] = (cos_u * sin_w + sin_u * cos_w).astype(jnp.bfloat16)
+
+        end = jnp.dot(end_q[...], cos_coeffs[...], preferred_element_type=jnp.float32)
+        end_flux = 0.5 * end[0:1, :LANES] * end[0:1, LANES:]
+
+        back_rows = back.reshape(2 * waves, LANES)
         pieces = 4
         owners = n_lat // pieces
-        high = total // pieces
-
-        @pl.loop(0, pieces)
-        def _(i):
-            piece = lax.rem(i + me // owners, pieces)
+        high = waves // pieces
+        scale = 2.0 / math.sqrt(LON)
+
+        target = ret.at[my_block, :, my_half, my_level]
+        my_piece = me // owners
+        my_place = lax.rem(me, owners)
+        for i in range(pieces):
+            piece = lax.rem(my_piece + 1 + i, pieces)
             rows = pl.ds(pl.multiple_of(piece * high, high), high)
-            zonal = jnp.dot(table_k[rows, :], flux[...], preferred_element_type=jnp.float32)
-            back_rows[rows, :] = (zonal * (1.0 / math.sqrt(LON))).astype(jnp.bfloat16)
-
-            @pl.loop(0, owners)
-            def _(j):
-                owner = piece * owners + lax.rem(j + me, owners)
-                target = ret.at[my_block, :, my_half, my_level]
-
-                @pl.when(owner != me)
-                def _():
-                    pltpu.make_async_remote_copy(
-                        src_ref=back.at[owner], dst_ref=target, send_sem=back_send_sem, recv_sem=back_recv_sem,
-                        device_id={"lat": owner}, device_id_type=mesh_id,
-                    ).start()
-
-                @pl.when(owner == me)
-                def _():
-                    pltpu.make_async_copy(back.at[owner], target, back_local_sem).start()
+            cos = jnp.dot(cos_k[rows, :], cos_flux[...], preferred_element_type=jnp.float32)
+            sin = jnp.dot(sin_k[rows, :], sin_flux[...], preferred_element_type=jnp.float32)
+            cos = cos + parity_of(row_waves[rows, :]) * end_flux
+            mix[i, pl.ds(0, high, 2), :] = cos * scale
+            mix[i, pl.ds(1, high, 2), :] = sin * scale
+            both = pl.ds(pl.multiple_of(piece * 2 * high, 2 * high), 2 * high)
+            back_rows[both, :] = mix[i].astype(jnp.bfloat16)
+            if i == pieces - 1:
+                pltpu.make_async_copy(back.at[me], target, back_local_sem).start()
+            for j in range(1 if i == pieces - 1 else 0, owners):
+                owner = piece * owners + lax.rem(my_place + j, owners)
+                pltpu.make_async_remote_copy(
+                    src_ref=back.at[owner], dst_ref=target, send_sem=back_send_sem, recv_sem=back_recv_sem,
+                    device_id={"lat": owner}, device_id_type=mesh_id,
+                ).start()
 
         pltpu.make_async_copy(back.at[me], back.at[me], back_local_sem).wait()
         sent = recv.at[:, pl.ds(0, units - 1)]
@@ -321,8 +351,7 @@
             device_id={"lev": partner}, device_id_type=mesh_id,
         )
 
-    @pl.loop(0, SLOTS)
-    def _(k):
+    for k in range(SLOTS):
         wave, parity, live, signed = factors(k)
         mixed = ret_rows[4, k].astype(jnp.float32)
         zero = jnp.zeros_like(mixed)
@@ -352,45 +381,54 @@
 def body(n_lat, assign, u_spec, v_spec, basis):
     slots, lev_dev, _, degrees = u_spec.shape
     half_rows = basis.shape[1]
-    order = jnp.repeat(assign.astype(jnp.float32), 2)
-    total = order.shape[0]
-    lane_waves = jnp.broadcast_to(order[None, :], (8, total))
+    waves = assign.shape[0]
     wide = 3 * LANES
 
     vmem = pl.BlockSpec(memory_space=pltpu.VMEM)
     smem = pl.BlockSpec(memory_space=pltpu.SMEM)
+    hbm = pl.BlockSpec(memory_space=pltpu.HBM)
     bf16 = jnp.bfloat16
+    f32 = jnp.float32
     dma = pltpu.SemaphoreType.DMA
     result = pl.pallas_call(
         functools.partial(kernel, n_lat, half_rows, degrees),
         out_shape=jax.ShapeDtypeStruct((slots, ROWS, degrees), jnp.float32),
-        in_specs=[smem, vmem, vmem, pl.BlockSpec(memory_space=pl.ANY), vmem],
+        in_specs=[smem, vmem, hbm, hbm, hbm],
         out_specs=vmem,
         scratch_shapes=[
             pltpu.VMEM((slots, wide, degrees), bf16),
+            pltpu.VMEM((slots, lev_dev, 2, degrees), bf16),
+            pltpu.VMEM((slots, lev_dev, 2, degrees), bf16),
             pltpu.VMEM((slots, lev_dev, 2, degrees), bf16),
             pltpu.VMEM((slots, lev_dev, 2, degrees), bf16),
             pltpu.VMEM((slots, 2, degrees), bf16),
             pltpu.VMEM((slots, 2, degrees), bf16),
             pltpu.VMEM((2, BLOCKS, SLOTS, 2, HALF_LEVELS, 2, LANES), bf16),
             pltpu.VMEM((2, n_lat, SLOTS, 2, LANES), bf16),
-            pltpu.VMEM((total, 2 * LANES), bf16),
-            pltpu.VMEM((LON, LANES), bf16),
+            pltpu.VMEM((2, 2 * waves, LANES), f32),
+            pltpu.VMEM((waves, 2 * LANES), bf16),
+            pltpu.VMEM((waves, 2 * LANES), bf16),
+            pltpu.VMEM((LON // 2, LANES), bf16),
+            pltpu.VMEM((LON // 2, LANES), bf16),
+            pltpu.VMEM((4, waves // 2, LANES), f32),
             pltpu.VMEM((n_lat, SLOTS, 2, LANES), bf16),
             pltpu.VMEM((BLOCKS, SLOTS, 2, HALF_LEVELS, 2, LANES), bf16),
             pltpu.VMEM((SLOTS, ROWS, degrees), bf16),
             pltpu.VMEM((SLOTS, ROWS, degrees), bf16),
-            pltpu.VMEM((LON, total), bf16),
-            pltpu.VMEM((total, LON), bf16),
-            pltpu.VMEM((total, LANES), jnp.float32),
+            pltpu.VMEM((LON // 2, waves), bf16),
+            pltpu.VMEM((LON // 2, waves), bf16),
+            pltpu.VMEM((ROWS, waves), bf16),
+            pltpu.VMEM((waves, LON // 2), bf16),
+            pltpu.VMEM((waves, LON // 2), bf16),
+            pltpu.VMEM((waves, LANES), f32),
             pltpu.SemaphoreType.REGULAR,
-            dma, dma((3,)), dma((3,)), dma((2,)), dma,
+            dma((3,)), dma((3,)), dma((3,)), dma((2,)), dma,
             dma, dma, dma, dma, dma, dma, dma((SLOTS,)), dma((SLOTS,)),
         ],
         compiler_params=pltpu.CompilerParams(
-            collective_id=0, has_side_effects=True, vmem_limit_bytes=48 * 1024 * 1024
+            collective_id=0, has_side_effects=True, vmem_limit_bytes=67043328
         ),
-    )(assign, u_spec, v_spec, basis, lane_waves)
+    )(assign, assign.reshape(waves // LANES, LANES), u_spec, v_spec, basis)
     return result.reshape(slots, lev_dev, 2, degrees)
 
 

time: 68.1 us -> 55.5 us (0.81)
  Pallas kernels: 64 us -> 53.6 us
  local copies, waits for them, and re-layouts: 3.07 us -> 1.72 us
  other arithmetic: 0.69 us -> 0 us
    pallas_call x1, Pallas kernels: 64 us -> 53.6 us  [body(): pl.pallas_call(functools.partial(kernel, n_lat, half_rows, degrees), out_...]
    unnamed x8 -> x0, local copies, waits for them, and re-layouts: 1.93 us -> none
    reshape x1, local copies, waits for them, and re-layouts: 0.79 us -> 1.72 us  [body(): return result.reshape(slots, lev_dev, 2, degrees)]
    convert_element_type x1 -> x0, other arithmetic: 0.69 us -> none  [body(): order = jnp.repeat(assign.astype(jnp.float32), 2)]
where the time goes in v3:
time: 55.5 us; the launch traced here: 55.3 us
  Pallas kernels  53.6 us (97%)
  local copies, waits for them, and re-layouts  1.72 us (3%)
    pallas_call x1, Pallas kernels, body(): pl.pallas_call(functools.partial(kernel, n_lat, half_rows, degrees), out_...  53.6 us
    reshape x1, local copies, waits for them, and re-layouts, body(): return result.reshape(slots, lev_dev, 2, degrees)  1.72 us

profile of v3, /device:TPU:6, one launch (start us, length us, event | category | flops | bytes accessed | tf_op | source)
XLA Modules:
  0.0 55.3 jit_solution(16574666324963722089)
XLA Ops:
  0.0 53.6 %shard_map.46 = f32[5,16,640]{2,1,0:T(8,128)} custom-call(s32[640]{0:T(1024)} %assign_ref.1, s32[5,128]{1,0:T(8,128)} %bitcast.1, bf16[5,8,2,640]{3,2,1,0:T(2,128)(2,1)} %u_ref.1, bf16[5,8,2,640]{3,2,1,0:T(2,128)(2,1)} %v_ref.1, bf16[5,160,640]{2,1,0:T(8,128)(2,1)} %basis_ref.1), custom_call_target="tpu_custom_call" | custom-call | tf_op jit(solution)/shard_map/pallas_call | solution.py:393
  53.6 1.7 %reshape.7 = f32[5,8,2,640]{3,2,1,0:T(2,128)} reshape(f32[5,16,640]{2,1,0:T(8,128)} %shard_map.46) | data formatting | bytes 409600 | tf_op jit(solution)/shard_map/reshape | solution.py:432

commit v4 on v3

--- a/solution.py
+++ b/solution.py
@@ -14,6 +14,7 @@
 LANES = 128
 GROUP = 16
 HALF_LEVELS = 8
+ORDER = (2, 1, 3, 0)
 ROWS = 16
 
 
@@ -39,13 +40,14 @@
 
 def kernel(
     n_lat, half_rows, degrees,
-    assign_ref, assign_lanes_ref, u_ref, v_ref, basis_ref,
-    out_ref,
+    assign_hbm, lanes_hbm, u_ref, v_ref, basis_ref,
+    out_hbm,
+    assign_ref, assign_lanes_ref, out_ref,
     wide_basis, u_own, v_own, u_other, v_other, edge_send, edge_recv,
     send, recv, split, cos_coeffs, sin_coeffs, cos_flux, sin_flux, mix, back, ret, sum_send, sum_recv,
     cos_q, sin_q, end_q, cos_k, sin_k, row_waves,
     ready, load_sem, swap_send_sem, swap_recv_sem, edge_send_sem, edge_recv_sem,
-    send_sem, recv_sem, local_sem, back_send_sem, back_recv_sem, back_local_sem, sum_send_sem, sum_recv_sem,
+    send_sem, recv_sem, local_sem, back_send_sem, back_recv_sem, back_local_sem, sum_send_sem, sum_recv_sem, out_sem,
 ):
     me = lax.axis_index("lat")
     lev = lax.axis_index("lev")
@@ -71,6 +73,8 @@
         pltpu.make_async_copy(basis_ref, wide_basis.at[:, own_rows], load_sem.at[0]),
         pltpu.make_async_copy(u_ref, u_own, load_sem.at[1]),
         pltpu.make_async_copy(v_ref, v_own, load_sem.at[2]),
+        pltpu.make_async_copy(assign_hbm, assign_ref, load_sem.at[3]),
+        pltpu.make_async_copy(lanes_hbm, assign_lanes_ref, load_sem.at[4]),
     ]
     for load in loads:
         load.start()
@@ -91,6 +95,19 @@
     def _(i):
         peer = lax.rem(me + i * GROUP, n_lat)
         pl.semaphore_signal(barrier, inc=1, device_id={"lat": peer}, device_id_type=mesh_id)
+
+    inner = x_hi + core == 1
+    loads[0].wait()
+
+    @pl.when(inner & (x_hi == 1))
+    def _():
+        for k in range(SLOTS):
+            edge_send[k] = jnp.broadcast_to(wide_basis[k, 0:ROWS, :][0:1], (2, degrees))
+
+    @pl.when(inner & (x_hi == 0))
+    def _():
+        for k in range(SLOTS):
+            edge_send[k] = jnp.broadcast_to(wide_basis[k, rows_x - ROWS : rows_x, :][ROWS - 1 :], (2, degrees))
 
     pl.semaphore_wait(barrier, 3 + GROUP - 1 + planes - 1)
 
@@ -103,19 +120,14 @@
             device_id={"lev": device}, device_id_type=mesh_id,
         )
 
-    swap_u = swap(0, u_own, u_other, partner)
-    swap_v = swap(1, v_own, v_other, partner)
-    swap_basis = swap(2, wide_basis.at[:, own_rows], wide_basis.at[:, own_rows], sibling)
-
-    @pl.loop(1, planes)
-    def _(i):
-        peer = lax.rem(me + i * GROUP, n_lat)
-        pl.semaphore_signal(ready, inc=1, device_id={"lat": peer}, device_id_type=mesh_id)
-
-    loads[0].wait()
-    swap_basis.start()
-
-    inner = x_hi + core == 1
+    groups = ((0, 3), (3, 2))
+    swaps = [
+        swap(2 * i + j, own.at[pl.ds(first, count)], other.at[pl.ds(first, count)], partner)
+        for i, (first, count) in enumerate(groups)
+        for j, (own, other) in enumerate(((u_own, u_other), (v_own, v_other)))
+    ]
+    swap_basis = swap(4, wide_basis.at[:, own_rows], wide_basis.at[:, own_rows], sibling)
+
     edge_base = 2 - 2 * x_hi
 
     def edge_copy(i):
@@ -124,25 +136,23 @@
             device_id={"lev": edge_base + i}, device_id_type=mesh_id,
         )
 
-    @pl.when(inner & (x_hi == 1))
-    def _():
-        for k in range(SLOTS):
-            edge_send[k] = jnp.broadcast_to(wide_basis[k, 0:ROWS, :][0:1], (2, degrees))
-
-    @pl.when(inner & (x_hi == 0))
-    def _():
-        for k in range(SLOTS):
-            edge_send[k] = jnp.broadcast_to(wide_basis[k, rows_x - ROWS : rows_x, :][ROWS - 1 :], (2, degrees))
-
     @pl.when(inner)
     def _():
         edge_copy(0).start()
         edge_copy(1).start()
 
+    swap_basis.start()
+    @pl.loop(1, planes)
+    def _(i):
+        peer = lax.rem(me + i * GROUP, n_lat)
+        pl.semaphore_signal(ready, inc=1, device_id={"lat": peer}, device_id_type=mesh_id)
+
     loads[1].wait()
-    swap_u.start()
     loads[2].wait()
-    swap_v.start()
+    for copy in swaps:
+        copy.start()
+    loads[3].wait()
+    loads[4].wait()
 
     lane_waves = []
     for t in range(waves // LANES):
@@ -185,8 +195,8 @@
         live = jnp.where(degree >= wave, 1.0, 0.0)
         return wave, parity, live, live * (parity * degree_sign)
 
-    def meridional(half, u_rows, v_rows):
-        for k in range(SLOTS):
+    def meridional(half, u_rows, v_rows, first, count):
+        for k in range(first, first + count):
             wave, parity, live, signed = factors(k)
             live = tile_rows(live, 2).astype(jnp.bfloat16)
             signed = tile_rows(signed, 2).astype(jnp.bfloat16)
@@ -216,6 +226,7 @@
                 for b, tile in enumerate(tiles):
                     send_rows[f, b, k, half] = tile.astype(jnp.bfloat16)
 
+    def send_half(half):
         def send_unit(block, group, level, turn):
             owner = group * 8 + lax.rem((8 * block) // 5 + turn, 8)
             return owner, pltpu.make_async_remote_copy(
@@ -227,30 +238,35 @@
             group = level * 2 + lax.rem(level + half, 2)
             return group, lax.rem(group * 3 + spread, 8)
 
-        group, turn = place(my_level)
-        for block in range(BLOCKS):
-            owner, copy = send_unit(block, group, my_level, turn)
-
-            @pl.when(owner != me)
-            def _():
-                copy.start()
-
-            @pl.when(owner == me)
-            def _():
-                pltpu.make_async_copy(send.at[:, block, :, half, my_level], recv.at[:, me], local_sem).start()
-
-        for i in range(1, HALF_LEVELS):
+        for i in (4, 3, 5, 2, 6, 1, 7):
             level = lax.rem(my_level + i, HALF_LEVELS)
             group, turn = place(level)
             for block in range(BLOCKS):
                 send_unit(block, group, level, turn)[1].start()
 
+        group, turn = place(my_level)
+        for block in range(BLOCKS):
+            owner, copy = send_unit(block, group, my_level, turn)
+
+            @pl.when(owner != me)
+            def _():
+                copy.start()
+
+            @pl.when(owner == me)
+            def _():
+                pltpu.make_async_copy(send.at[:, block, :, half, my_level], recv.at[:, me], local_sem).start()
+
+    meridional(0, u_own.reshape(SLOTS, ROWS, degrees), v_own.reshape(SLOTS, ROWS, degrees), 0, SLOTS)
     pl.semaphore_wait(ready, planes - 1)
-    meridional(0, u_own.reshape(SLOTS, ROWS, degrees), v_own.reshape(SLOTS, ROWS, degrees))
-
-    swap_u.wait()
-    swap_v.wait()
-    meridional(1, u_other.reshape(SLOTS, ROWS, degrees), v_other.reshape(SLOTS, ROWS, degrees))
+    send_half(0)
+
+    for i, (first, count) in enumerate(groups):
+        swaps[2 * i].wait()
+        swaps[2 * i + 1].wait()
+        meridional(
+            1, u_other.reshape(SLOTS, ROWS, degrees), v_other.reshape(SLOTS, ROWS, degrees), first, count
+        )
+    send_half(1)
 
     wave = jnp.concatenate(lane_waves, axis=1)
     end_q[...] = tile_rows(parity_of(wave), ROWS // 8).astype(jnp.bfloat16)
@@ -283,7 +299,7 @@
             split[f] = recv_rows[f].astype(jnp.float32)
             cos_coeffs[:, lanes] = split[f, pl.ds(0, waves, 2), :].astype(jnp.bfloat16)
             sin_coeffs[:, lanes] = split[f, pl.ds(1, waves, 2), :].astype(jnp.bfloat16)
-        step = 256
+        step = 640
         first_row = lax.broadcasted_iota(jnp.int32, (step, LANES), 0)
 
         @pl.loop(0, half_lon // step)
@@ -301,7 +317,7 @@
         end_flux = 0.5 * end[0:1, :LANES] * end[0:1, LANES:]
 
         back_rows = back.reshape(2 * waves, LANES)
-        pieces = 4
+        pieces = len(ORDER)
         owners = n_lat // pieces
         high = waves // pieces
         scale = 2.0 / math.sqrt(LON)
@@ -309,8 +325,8 @@
         target = ret.at[my_block, :, my_half, my_level]
         my_piece = me // owners
         my_place = lax.rem(me, owners)
-        for i in range(pieces):
-            piece = lax.rem(my_piece + 1 + i, pieces)
+        for i, offset in enumerate(ORDER):
+            piece = lax.rem(my_piece + offset, pieces)
             rows = pl.ds(pl.multiple_of(piece * high, high), high)
             cos = jnp.dot(cos_k[rows, :], cos_flux[...], preferred_element_type=jnp.float32)
             sin = jnp.dot(sin_k[rows, :], sin_flux[...], preferred_element_type=jnp.float32)
@@ -341,6 +357,7 @@
         got = recv.at[0, pl.ds(0, units)]
         pltpu.make_async_copy(got, got, back_recv_sem).wait()
 
+    out_rows = out_ref.reshape(SLOTS, ROWS, degrees)
     ret_rows = ret.reshape(BLOCKS, SLOTS, 2 * ROWS, LANES)
     wide_lane = lax.broadcasted_iota(jnp.int32, (2 * ROWS, LANES), 1)
 
@@ -365,17 +382,20 @@
         combined = tile_rows(live, 4) * both[: 2 * ROWS] + tile_rows(signed, 4) * both[2 * ROWS :]
         sum_send[k] = combined[ROWS:].astype(jnp.bfloat16)
         sum_copy(k).start()
-        out_ref[k] = combined[:ROWS]
+        out_rows[k] = combined[:ROWS]
 
     @pl.when(active)
     def _():
         sent = recv.at[0, pl.ds(0, n_lat - 1)]
         pltpu.make_async_copy(sent, sent, back_send_sem).wait()
 
-    @pl.loop(0, SLOTS)
-    def _(k):
+    stores = [pltpu.make_async_copy(out_ref.at[k], out_hbm.at[k], out_sem.at[k]) for k in range(SLOTS)]
+    for k in range(SLOTS):
         sum_copy(k).wait()
-        out_ref[k] += sum_recv[k].astype(jnp.float32)
+        out_rows[k] += sum_recv[k].astype(jnp.float32)
+        stores[k].start()
+    for store in stores:
+        store.wait()
 
 
 def body(n_lat, assign, u_spec, v_spec, basis):
@@ -384,18 +404,19 @@
     waves = assign.shape[0]
     wide = 3 * LANES
 
-    vmem = pl.BlockSpec(memory_space=pltpu.VMEM)
-    smem = pl.BlockSpec(memory_space=pltpu.SMEM)
     hbm = pl.BlockSpec(memory_space=pltpu.HBM)
     bf16 = jnp.bfloat16
     f32 = jnp.float32
     dma = pltpu.SemaphoreType.DMA
     result = pl.pallas_call(
         functools.partial(kernel, n_lat, half_rows, degrees),
-        out_shape=jax.ShapeDtypeStruct((slots, ROWS, degrees), jnp.float32),
-        in_specs=[smem, vmem, hbm, hbm, hbm],
-        out_specs=vmem,
+        out_shape=jax.ShapeDtypeStruct((slots, lev_dev, 2, degrees), jnp.float32),
+        in_specs=[hbm] * 5,
+        out_specs=hbm,
         scratch_shapes=[
+            pltpu.SMEM((waves,), jnp.int32),
+            pltpu.VMEM((waves // LANES, LANES), jnp.int32),
+            pltpu.VMEM((slots, lev_dev, 2, degrees), f32),
             pltpu.VMEM((slots, wide, degrees), bf16),
             pltpu.VMEM((slots, lev_dev, 2, degrees), bf16),
             pltpu.VMEM((slots, lev_dev, 2, degrees), bf16),
@@ -410,7 +431,7 @@
             pltpu.VMEM((waves, 2 * LANES), bf16),
             pltpu.VMEM((LON // 2, LANES), bf16),
             pltpu.VMEM((LON // 2, LANES), bf16),
-            pltpu.VMEM((4, waves // 2, LANES), f32),
+            pltpu.VMEM((len(ORDER), 2 * waves // len(ORDER), LANES), f32),
             pltpu.VMEM((n_lat, SLOTS, 2, LANES), bf16),
             pltpu.VMEM((BLOCKS, SLOTS, 2, HALF_LEVELS, 2, LANES), bf16),
             pltpu.VMEM((SLOTS, ROWS, degrees), bf16),
@@ -422,14 +443,14 @@
             pltpu.VMEM((waves, LON // 2), bf16),
             pltpu.VMEM((waves, LANES), f32),
             pltpu.SemaphoreType.REGULAR,
-            dma((3,)), dma((3,)), dma((3,)), dma((2,)), dma,
-            dma, dma, dma, dma, dma, dma, dma((SLOTS,)), dma((SLOTS,)),
+            dma((5,)), dma((5,)), dma((5,)), dma((2,)), dma,
+            dma, dma, dma, dma, dma, dma, dma((SLOTS,)), dma((SLOTS,)), dma((SLOTS,)),
         ],
         compiler_params=pltpu.CompilerParams(
             collective_id=0, has_side_effects=True, vmem_limit_bytes=67043328
         ),
     )(assign, assign.reshape(waves // LANES, LANES), u_spec, v_spec, basis)
-    return result.reshape(slots, lev_dev, 2, degrees)
+    return result
 
 
 def solution(mesh):

time: 55.5 us -> 52.6 us (0.948)
  Pallas kernels: 53.6 us -> 50.7 us
    pallas_call x1, Pallas kernels: 53.6 us -> 50.7 us  [body(): pl.pallas_call(functools.partial(kernel, n_lat, half_rows, degrees), out_...]
    reshape x1 -> x0, local copies, waits for them, and re-layouts: 1.72 us -> none  [body(): return result.reshape(slots, lev_dev, 2, degrees)]
    unnamed x0 -> x1, local copies, waits for them, and re-layouts: none -> 1.64 us
where the time goes in v4:
time: 52.6 us; the launch traced here: 52.4 us
  Pallas kernels  50.7 us (96%)
  local copies, waits for them, and re-layouts  1.64 us (3%)
    pallas_call x1, Pallas kernels, body(): pl.pallas_call(functools.partial(kernel, n_lat, half_rows, degrees), out_...  50.7 us
    unnamed x1, local copies, waits for them, and re-layouts  1.64 us

profile of v4, /device:TPU:6, one launch (start us, length us, event | category | flops | bytes accessed | tf_op | source)
XLA Modules:
  0.0 52.4 jit_solution(14871663411319270470)
XLA Ops:
  0.0 50.7 %shard_map.46 = f32[5,8,2,640]{3,2,1,0:T(2,128)} custom-call(s32[640]{0:T(1024)} %assign_hbm.1, s32[5,128]{1,0:T(8,128)} %bitcast.1, bf16[5,8,2,640]{3,2,1,0:T(2,128)(2,1)} %u_ref.1, bf16[5,8,2,640]{3,2,1,0:T(2,128)(2,1)} %v_ref.1, bf16[5,160,640]{2,1,0:T(8,128)(2,1)} %basis_ref.1), custom_call_target="tpu_custom_call" | custom-call | tf_op jit(solution)/shard_map/pallas_call | solution.py:411
  50.7 1.6 %copy.6 = f32[5,8,2,640]{3,2,1,0:T(2,128)} copy(f32[5,8,2,640]{3,2,1,0:T(2,128)} %shard_map.46) | data formatting | bytes 409600

commit v5 on v4

--- a/solution.py
+++ b/solution.py
@@ -41,10 +41,10 @@
 def kernel(
     n_lat, half_rows, degrees,
     assign_hbm, lanes_hbm, u_ref, v_ref, basis_ref,
-    out_hbm,
+    out_hbm, sum_hbm,
     assign_ref, assign_lanes_ref, out_ref,
     wide_basis, u_own, v_own, u_other, v_other, edge_send, edge_recv,
-    send, recv, split, cos_coeffs, sin_coeffs, cos_flux, sin_flux, mix, back, ret, sum_send, sum_recv,
+    send, recv, split, cos_coeffs, sin_coeffs, cos_flux, sin_flux, mix, back, ret, sum_send,
     cos_q, sin_q, end_q, cos_k, sin_k, row_waves,
     ready, load_sem, swap_send_sem, swap_recv_sem, edge_send_sem, edge_recv_sem,
     send_sem, recv_sem, local_sem, back_send_sem, back_recv_sem, back_local_sem, sum_send_sem, sum_recv_sem, out_sem,
@@ -53,7 +53,6 @@
     lev = lax.axis_index("lev")
     x_hi = lev // 2
     core = lax.rem(lev, 2)
-    spread = 2 * lev
     rows_x = 2 * half_rows
     wide = wide_basis.shape[1]
     waves = SLOTS * n_lat
@@ -61,12 +60,14 @@
     units = BLOCKS * GROUP
     mesh_id = pl.DeviceIdType.MESH
 
-    my_group = me // 8
-    my_z = lax.rem(lax.rem(me, 8) + 32 - lax.rem(my_group * 3 + spread, 8), 8)
+    def turn_of(level):
+        return lax.rem(5 * level + 4 * core, 8)
+
+    my_level = me // GROUP
+    my_z = lax.rem(lax.rem(me, 8) + 8 - turn_of(my_level), 8)
     my_block = (5 * my_z + 7) // 8
     active = (8 * my_block) // 5 == my_z
-    my_level = my_group // 2
-    my_half = lax.rem(my_group + my_level, 2)
+    my_half = lax.rem(lax.rem(me // 8, 2) + my_block + my_level, 2)
 
     own_rows = pl.ds(pl.multiple_of(core * half_rows, ROWS), half_rows)
     loads = [
@@ -227,26 +228,26 @@
                     send_rows[f, b, k, half] = tile.astype(jnp.bfloat16)
 
     def send_half(half):
-        def send_unit(block, group, level, turn):
-            owner = group * 8 + lax.rem((8 * block) // 5 + turn, 8)
+        def send_unit(block, level, sides, turn):
+            owner = sides[block % 2] + lax.rem((8 * block) // 5 + turn, 8)
             return owner, pltpu.make_async_remote_copy(
                 src_ref=send.at[:, block, :, half, level], dst_ref=recv.at[:, me], send_sem=send_sem, recv_sem=recv_sem,
                 device_id={"lat": owner}, device_id_type=mesh_id,
             )
 
         def place(level):
-            group = level * 2 + lax.rem(level + half, 2)
-            return group, lax.rem(group * 3 + spread, 8)
+            sides = [level * GROUP + 8 * lax.rem(level + half + p, 2) for p in range(2)]
+            return sides, turn_of(level)
 
         for i in (4, 3, 5, 2, 6, 1, 7):
             level = lax.rem(my_level + i, HALF_LEVELS)
-            group, turn = place(level)
+            sides, turn = place(level)
             for block in range(BLOCKS):
-                send_unit(block, group, level, turn)[1].start()
-
-        group, turn = place(my_level)
+                send_unit(block, level, sides, turn)[1].start()
+
+        sides, turn = place(my_level)
         for block in range(BLOCKS):
-            owner, copy = send_unit(block, group, my_level, turn)
+            owner, copy = send_unit(block, my_level, sides, turn)
 
             @pl.when(owner != me)
             def _():
@@ -358,12 +359,14 @@
         pltpu.make_async_copy(got, got, back_recv_sem).wait()
 
     out_rows = out_ref.reshape(SLOTS, ROWS, degrees)
+    sum_rows = sum_send.reshape(SLOTS, ROWS, degrees)
+    stores = [pltpu.make_async_copy(out_ref.at[k], out_hbm.at[k], out_sem.at[k]) for k in range(SLOTS)]
     ret_rows = ret.reshape(BLOCKS, SLOTS, 2 * ROWS, LANES)
     wide_lane = lax.broadcasted_iota(jnp.int32, (2 * ROWS, LANES), 1)
 
     def sum_copy(k):
         return pltpu.make_async_remote_copy(
-            src_ref=sum_send.at[k], dst_ref=sum_recv.at[k],
+            src_ref=sum_send.at[k], dst_ref=sum_hbm.at[k],
             send_sem=sum_send_sem.at[k], recv_sem=sum_recv_sem.at[k],
             device_id={"lev": partner}, device_id_type=mesh_id,
         )
@@ -380,22 +383,20 @@
             jnp.concatenate([north, south], axis=0), wide_basis[k], preferred_element_type=jnp.float32
         )
         combined = tile_rows(live, 4) * both[: 2 * ROWS] + tile_rows(signed, 4) * both[2 * ROWS :]
-        sum_send[k] = combined[ROWS:].astype(jnp.bfloat16)
+        sum_rows[k] = combined[ROWS:].astype(jnp.bfloat16)
         sum_copy(k).start()
         out_rows[k] = combined[:ROWS]
+        stores[k].start()
 
     @pl.when(active)
     def _():
         sent = recv.at[0, pl.ds(0, n_lat - 1)]
         pltpu.make_async_copy(sent, sent, back_send_sem).wait()
 
-    stores = [pltpu.make_async_copy(out_ref.at[k], out_hbm.at[k], out_sem.at[k]) for k in range(SLOTS)]
+    for k in range(SLOTS):
+        stores[k].wait()
     for k in range(SLOTS):
         sum_copy(k).wait()
-        out_rows[k] += sum_recv[k].astype(jnp.float32)
-        stores[k].start()
-    for store in stores:
-        store.wait()
 
 
 def body(n_lat, assign, u_spec, v_spec, basis):
@@ -408,11 +409,11 @@
     bf16 = jnp.bfloat16
     f32 = jnp.float32
     dma = pltpu.SemaphoreType.DMA
-    result = pl.pallas_call(
+    own, other = pl.pallas_call(
         functools.partial(kernel, n_lat, half_rows, degrees),
-        out_shape=jax.ShapeDtypeStruct((slots, lev_dev, 2, degrees), jnp.float32),
+        out_shape=[jax.ShapeDtypeStruct(u_spec.shape, f32), jax.ShapeDtypeStruct(u_spec.shape, bf16)],
         in_specs=[hbm] * 5,
-        out_specs=hbm,
+        out_specs=[hbm, hbm],
         scratch_shapes=[
             pltpu.SMEM((waves,), jnp.int32),
             pltpu.VMEM((waves // LANES, LANES), jnp.int32),
@@ -434,8 +435,7 @@
             pltpu.VMEM((len(ORDER), 2 * waves // len(ORDER), LANES), f32),
             pltpu.VMEM((n_lat, SLOTS, 2, LANES), bf16),
             pltpu.VMEM((BLOCKS, SLOTS, 2, HALF_LEVELS, 2, LANES), bf16),
-            pltpu.VMEM((SLOTS, ROWS, degrees), bf16),
-            pltpu.VMEM((SLOTS, ROWS, degrees), bf16),
+            pltpu.VMEM((slots, lev_dev, 2, degrees), bf16),
             pltpu.VMEM((LON // 2, waves), bf16),
             pltpu.VMEM((LON // 2, waves), bf16),
             pltpu.VMEM((ROWS, waves), bf16),
@@ -450,7 +450,7 @@
             collective_id=0, has_side_effects=True, vmem_limit_bytes=67043328
         ),
     )(assign, assign.reshape(waves // LANES, LANES), u_spec, v_spec, basis)
-    return result
+    return own + other.astype(f32)
 
 
 def solution(mesh):

time: 52.6 us -> 51.1 us (0.971)
  Pallas kernels: 50.7 us -> 49 us
  other arithmetic: 0 us -> 1.7 us
  local copies, waits for them, and re-layouts: 1.64 us -> 0 us
    pallas_call x1, Pallas kernels: 50.7 us -> 49 us  [body(): pl.pallas_call(functools.partial(kernel, n_lat, half_rows, degrees), out_...]
    add x0 -> x1, other arithmetic: none -> 1.7 us  [body(): return own + other.astype(f32)]
    unnamed x1 -> x0, local copies, waits for them, and re-layouts: 1.64 us -> none
where the time goes in v5:
time: 51.1 us; the launch traced here: 50.7 us
  Pallas kernels  49 us (96%)
  other arithmetic  1.7 us (3%)
    pallas_call x1, Pallas kernels, body(): pl.pallas_call(functools.partial(kernel, n_lat, half_rows, degrees), out_...  49 us
    add x1, other arithmetic, body(): return own + other.astype(f32)  1.7 us

profile of v5, /device:TPU:6, one launch (start us, length us, event | category | flops | bytes accessed | tf_op | source)
XLA Modules:
  0.0 50.7 jit_solution(301389346420008233)
XLA Ops:
  0.0 49.0 %shard_map.46 = (f32[5,8,2,640]{3,2,1,0:T(2,128)}, bf16[5,8,2,640]{3,2,1,0:T(2,128)(2,1)}) custom-call(s32[640]{0:T(1024)} %assign_hbm.1, s32[5,128]{1,0:T(8,128)} %bitcast.6, bf16[5,8,2,640]{3,2,1,0:T(2,128)(2,1)} %u_ref.1, bf16[5,8,2,640]{3,2,1,0:T(2,128)(2,1)} %v_ref.1, bf16[5,160,640]{2,1,0:T(8,128)(2,1)} %basis_ref.1), custom_call_target="tpu_custom_call" | custom-call | tf_op jit(solution)/shard_map/pallas_call | solution.py:412
  49.0 1.7 %convert_add_fusion = f32[5,2,8,640]{3,2,1,0:T(8,128)} fusion(f32[5,2,8,640]{3,2,1,0:T(8,128)} %bitcast.4, bf16[5,2,8,640]{3,2,1,0:T(8,128)(2,1)} %bitcast.5), kind=kLoop, calls=%fused_computation | loop fusion | flops 102400 | bytes 512000 | tf_op jit(solution)/shard_map/add | solution.py:453

commit v6 on v5

--- a/solution.py
+++ b/solution.py
@@ -300,7 +300,7 @@
             split[f] = recv_rows[f].astype(jnp.float32)
             cos_coeffs[:, lanes] = split[f, pl.ds(0, waves, 2), :].astype(jnp.bfloat16)
             sin_coeffs[:, lanes] = split[f, pl.ds(1, waves, 2), :].astype(jnp.bfloat16)
-        step = 640
+        step = 1280
         first_row = lax.broadcasted_iota(jnp.int32, (step, LANES), 0)
 
         @pl.loop(0, half_lon // step)
@@ -339,7 +339,7 @@
             if i == pieces - 1:
                 pltpu.make_async_copy(back.at[me], target, back_local_sem).start()
             for j in range(1 if i == pieces - 1 else 0, owners):
-                owner = piece * owners + lax.rem(my_place + j, owners)
+                owner = piece * owners + lax.rem(my_place + j + (GROUP if i < 2 else 0), owners)
                 pltpu.make_async_remote_copy(
                     src_ref=back.at[owner], dst_ref=target, send_sem=back_send_sem, recv_sem=back_recv_sem,
                     device_id={"lat": owner}, device_id_type=mesh_id,

time: 51.1 us -> 50.6 us (level)
  no operation moved by 1% of the time
where the time goes in v6:
time: 50.6 us; the launch traced here: 50.4 us
  Pallas kernels  48.7 us (96%)
  other arithmetic  1.7 us (3%)
    pallas_call x1, Pallas kernels, body(): pl.pallas_call(functools.partial(kernel, n_lat, half_rows, degrees), out_...  48.7 us
    add x1, other arithmetic, body(): return own + other.astype(f32)  1.7 us

profile of v6, /device:TPU:6, one launch (start us, length us, event | category | flops | bytes accessed | tf_op | source)
XLA Modules:
  0.0 50.4 jit_solution(13303455267670405604)
XLA Ops:
  0.0 48.7 %shard_map.46 = (f32[5,8,2,640]{3,2,1,0:T(2,128)}, bf16[5,8,2,640]{3,2,1,0:T(2,128)(2,1)}) custom-call(s32[640]{0:T(1024)} %assign_hbm.1, s32[5,128]{1,0:T(8,128)} %bitcast.6, bf16[5,8,2,640]{3,2,1,0:T(2,128)(2,1)} %u_ref.1, bf16[5,8,2,640]{3,2,1,0:T(2,128)(2,1)} %v_ref.1, bf16[5,160,640]{2,1,0:T(8,128)(2,1)} %basis_ref.1), custom_call_target="tpu_custom_call" | custom-call | tf_op jit(solution)/shard_map/pallas_call | solution.py:412
  48.7 1.7 %convert_add_fusion = f32[5,2,8,640]{3,2,1,0:T(8,128)} fusion(f32[5,2,8,640]{3,2,1,0:T(8,128)} %bitcast.4, bf16[5,2,8,640]{3,2,1,0:T(8,128)(2,1)} %bitcast.5), kind=kLoop, calls=%fused_computation | loop fusion | flops 102400 | bytes 512000 | tf_op jit(solution)/shard_map/add | solution.py:453

commit v7 on v6

--- a/solution.py
+++ b/solution.py
@@ -121,7 +121,7 @@
             device_id={"lev": device}, device_id_type=mesh_id,
         )
 
-    groups = ((0, 3), (3, 2))
+    groups = ((0, 4), (4, 1))
     swaps = [
         swap(2 * i + j, own.at[pl.ds(first, count)], other.at[pl.ds(first, count)], partner)
         for i, (first, count) in enumerate(groups)
@@ -239,7 +239,7 @@
             sides = [level * GROUP + 8 * lax.rem(level + half + p, 2) for p in range(2)]
             return sides, turn_of(level)
 
-        for i in (4, 3, 5, 2, 6, 1, 7):
+        for i in ((4, 3, 5, 2, 6, 1, 7) if half == 0 else (4, 5, 3, 6, 2, 7, 1)):
             level = lax.rem(my_level + i, HALF_LEVELS)
             sides, turn = place(level)
             for block in range(BLOCKS):

time: 50.6 us -> 50.6 us (level)
  no operation moved by 1% of the time
where the time goes in v7:
time: 50.6 us; the launch traced here: 50.4 us
  Pallas kernels  48.7 us (96%)
  other arithmetic  1.7 us (3%)
    pallas_call x1, Pallas kernels, body(): pl.pallas_call(functools.partial(kernel, n_lat, half_rows, degrees), out_...  48.7 us
    add x1, other arithmetic, body(): return own + other.astype(f32)  1.7 us

profile of v7, /device:TPU:6, one launch (start us, length us, event | category | flops | bytes accessed | tf_op | source)
XLA Modules:
  0.0 50.4 jit_solution(4850293393439046785)
XLA Ops:
  0.0 48.7 %shard_map.46 = (f32[5,8,2,640]{3,2,1,0:T(2,128)}, bf16[5,8,2,640]{3,2,1,0:T(2,128)(2,1)}) custom-call(s32[640]{0:T(1024)} %assign_hbm.1, s32[5,128]{1,0:T(8,128)} %bitcast.6, bf16[5,8,2,640]{3,2,1,0:T(2,128)(2,1)} %u_ref.1, bf16[5,8,2,640]{3,2,1,0:T(2,128)(2,1)} %v_ref.1, bf16[5,160,640]{2,1,0:T(8,128)(2,1)} %basis_ref.1), custom_call_target="tpu_custom_call" | custom-call | tf_op jit(solution)/shard_map/pallas_call | solution.py:412
  48.7 1.7 %convert_add_fusion = f32[5,2,8,640]{3,2,1,0:T(8,128)} fusion(f32[5,2,8,640]{3,2,1,0:T(8,128)} %bitcast.4, bf16[5,2,8,640]{3,2,1,0:T(8,128)(2,1)} %bitcast.5), kind=kLoop, calls=%fused_computation | loop fusion | flops 102400 | bytes 512000 | tf_op jit(solution)/shard_map/add | solution.py:453
